TPU v7x, 32 devices: a whole 2x2x4 slice. The times are simulated.
32 devices in a mesh: dp: 8 (over y, x, core), mp: 4 (over z).
Axes of the slice: x: 2, y: 2, z: 4, core: 2. Of those that a mesh axis runs over, the one named last changes fastest.
Arguments:
- feature_ids: int32 [8, 2048, 8], P('dp'), may hold values from 0 to 4095
- tables: bfloat16 [8, 4096, 128], P('dp'), may hold values from -5 to 5
- table_of_feature: int32 [8], replicated, may hold values from 0 to 7, each once
- cross_down: bfloat16 [2, 1024, 512], P(None, 'mp'), may hold values from -0.1875 to 0.1875
- cross_up: bfloat16 [2, 1024, 512], P(None, 'mp'), may hold values from -0.125 to 0.125
- cross_bias: float32 [2, 1024], P(None, 'mp'), may hold values from -3 to 3
- tower_weight: bfloat16 [1024, 2048], P('dp', 'mp'), may hold values from -0.1875 to 0.1875
- tower_bias: float32 [2048], P('mp'), may hold values from -3 to 3
Outputs:
- hidden: bfloat16 [2048, 2048], P('dp', 'mp')
Inputs may be any that keep to these rules, and one draw needn't show every extreme that they name: `feature_ids`: each id indexes a row of its own table. `table_of_feature`: each table serves exactly one feature.
All inputs are finite; a program needn't handle non-finite values.
Results may differ from a plain program's by a relative error of at most 0.015.
Values may be sent and summed in bfloat16 or wider, within the bound.
A program may use at most 64 MiB of HBM per device.

v0:
```python
import functools

import jax
import jax.numpy as jnp
from jax import lax
from jax.experimental import pallas as pl
from jax.experimental.pallas import tpu as pltpu
from jax.sharding import PartitionSpec as P


def plain_body(
    feature_ids,
    tables,
    table_of_feature,
    cross_down,
    cross_up,
    cross_bias,
    tower_weight,
    tower_bias,
):
    groups = lax.axis_size("dp")
    members = lax.axis_size("mp")
    member = lax.axis_index("mp")
    table_count, batch_size, hot_count = feature_ids.shape
    row_count = batch_size // (groups * members)
    shaped = feature_ids[0].reshape(groups, members, row_count, hot_count)
    own_ids = lax.dynamic_index_in_dim(shaped, member, 1, keepdims=False).reshape(
        groups * row_count, hot_count
    )
    summed = jnp.zeros((groups * row_count, tables.shape[2]), jnp.float32)
    for hot_index in range(hot_count):
        summed = summed + jnp.take(tables[0], own_ids[:, hot_index], axis=0).astype(jnp.float32)
    columns = [summed.astype(jnp.bfloat16)]
    pooled = jnp.stack(columns, axis=1)
    regrouped = lax.all_to_all(pooled, "dp", split_axis=0, concat_axis=1, tiled=True)
    ordered = jnp.take(regrouped, table_of_feature, axis=1)
    by_width = lax.all_to_all(ordered, "mp", split_axis=1, concat_axis=0, tiled=True)
    group_rows = by_width.shape[0]
    embedded = by_width.reshape(group_rows, -1)
    embedded_wide = embedded.astype(jnp.float32)
    crossed = embedded
    layer_total = cross_down.shape[0]
    for layer_index in range(layer_total):
        partial_value = jnp.dot(
            crossed, cross_down[layer_index], preferred_element_type=jnp.float32
        )
        projected = lax.psum(partial_value.astype(jnp.bfloat16), "mp")
        lifted = lax.dot_general(
            projected,
            cross_up[layer_index],
            (((1,), (1,)), ((), ())),
            preferred_element_type=jnp.float32,
        )
        crossed = (
            embedded_wide * (lifted + cross_bias[layer_index]) + crossed.astype(jnp.float32)
        ).astype(jnp.bfloat16)
    full_rows = lax.all_gather(crossed, "mp", axis=1, tiled=True)
    pre_act = jnp.dot(
        full_rows,
        lax.all_gather(tower_weight, "dp", axis=0, tiled=True),
        preferred_element_type=jnp.float32,
    )
    return jax.nn.relu(pre_act + tower_bias).astype(jnp.bfloat16)


MESH = pl.DeviceIdType.MESH
KERNEL_BYTES = 24 * 1024 * 1024
VMEM_BYTES = (64 * 1024 - 352) * 1024
CHIPS = 4


def kernel(
    groups,
    members,
    ids_hbm,
    order_hbm,
    table,
    down,
    up,
    bias,
    tower,
    tower_bias_hbm,
    out,
    ids,
    order,
    table_half,
    table_wide,
    sums,
    outbox,
    pooled,
    embedded,
    crossed,
    weights,
    biases,
    tower_all,
    tower_bias,
    crossed_all,
    local_sem,
    z_send,
    z_recv,
    plane_send,
    plane_recv,
    diag_send,
    diag_recv,
    pair_send,
    pair_recv,
    bias_send,
    bias_recv,
    t_plane_send,
    t_plane_recv,
    t_diag_send,
    t_diag_recv,
    t_pair_send,
    t_pair_recv,
    pool_send,
    pool_recv,
    cross_send,
    cross_recv,
):
    d = lax.axis_index("dp")
    m = lax.axis_index("mp")
    q = lax.div(d, 2)
    c = lax.rem(d, 2)
    partner = q * 2 + 1 - c
    chip_x = q + 1 - 2 * lax.rem(q, 2)
    chip_y = lax.rem(q + 2, CHIPS)
    chip_z = lax.rem(chip_x + 2, CHIPS)
    chips = (chip_x, chip_y, chip_z)
    layers, block, rank = down.shape
    hots = ids.shape[0]
    rows, embed = sums.shape
    piece = block // groups
    depth = tower.shape[0]
    pieces = 2 * layers
    sends = []
    locals_ = []

    def wrap(value, size):
        return lax.rem(value + size, size)

    def load(src, dst):
        copy = pltpu.make_async_copy(src, dst, local_sem.at[len(locals_)])
        copy.start()
        locals_.append(copy)
        return copy

    def send(src, dst, send_sem, recv_sem, to_d, to_m):
        copy = pltpu.make_async_remote_copy(
            src_ref=src,
            dst_ref=dst,
            send_sem=send_sem,
            recv_sem=recv_sem,
            device_id=(to_d, to_m),
            device_id_type=MESH,
        )
        copy.start()
        sends.append(copy)

    def arrived(ref, send_sem, recv_sem):
        pltpu.make_async_remote_copy(
            src_ref=ref,
            dst_ref=ref,
            send_sem=send_sem,
            recv_sem=recv_sem,
            device_id=(partner, m),
            device_id_type=MESH,
        ).wait_recv()

    def came(k):
        return wrap(m - k, members)

    def goes(k):
        return wrap(m + k, members)

    def slot(p, member, device, half=None):
        length = piece if half is None else piece // 2
        start = member * block + device * piece + (0 if half is None else half * length)
        return weights.at[p, pl.ds(pl.multiple_of(start, length), length), :]

    def tower_slot(device, half=None):
        length = depth if half is None else depth // 2
        start = device * depth + (0 if half is None else half * length)
        return tower_all.at[pl.ds(pl.multiple_of(start, length), length), :]

    def source(p):
        return (down, up)[p % 2].at[p // 2]

    barrier = pltpu.get_barrier_semaphore()
    for k in range(1, members):
        pl.semaphore_signal(barrier, inc=1, device_id=(d, goes(k)), device_id_type=MESH)
    for i in range(1, groups):
        pl.semaphore_signal(barrier, inc=1, device_id=(wrap(d + i, groups), m), device_id_type=MESH)

    ids_copy = load(ids_hbm, ids)
    table_copy = load(table.at[0], table_half)
    weight_copies = []
    for p in range(pieces):
        here = pl.ds(pl.multiple_of(m * block, block), block)
        weight_copies.append(load(source(p), weights.at[p, here, :]))
    bias_copy = load(bias, biases.at[m])
    order_copy = load(order_hbm, order)
    tower_copy = load(tower, tower_slot(d))
    tower_bias_copy = load(tower_bias_hbm, tower_bias)

    def spread(p):
        for k in range(1, members):
            here = slot(p, came(k), d)
            arrived(here, z_send.at[p, k], z_recv.at[p, k])
            send(here, here, plane_send.at[p, k, 0], plane_recv.at[p, k, 0], chip_x * 2 + c, m)
            send(here, here, plane_send.at[p, k, 1], plane_recv.at[p, k, 1], chip_y * 2 + c, m)
            send(here, here, plane_send.at[p, k, 2], plane_recv.at[p, k, 2], partner, m)

    def relay(p):
        for k in range(1, members):
            for j in range(2):
                chip = chips[j]
                here = slot(p, came(k), chip * 2 + c)
                arrived(here, plane_send.at[p, k, j], plane_recv.at[p, k, j])
                half = slot(p, came(k), chip * 2 + c, j)
                send(
                    half,
                    half,
                    diag_send.at[p, k, j],
                    diag_recv.at[p, k, j],
                    chips[1 - j] * 2 + c,
                    m,
                )
                send(here, here, pair_send.at[p, k, j], pair_recv.at[p, k, j], partner, m)

    def finish_diag(p, k):
        for j in range(2):
            half = slot(p, came(k), chip_z * 2 + c, j)
            arrived(half, diag_send.at[p, k, j], diag_recv.at[p, k, j])
        here = slot(p, came(k), chip_z * 2 + c)
        send(here, here, pair_send.at[p, k, 2], pair_recv.at[p, k, 2], partner, m)

    def diag(p):
        for k in range(1, members):
            finish_diag(p, k)

    def complete(p, k):
        if k == 0:
            weight_copies[p].wait()
            return
        here = slot(p, came(k), partner)
        arrived(here, plane_send.at[p, k, 2], plane_recv.at[p, k, 2])
        for j in range(3):
            here = slot(p, came(k), chips[j] * 2 + 1 - c)
            arrived(here, pair_send.at[p, k, j], pair_recv.at[p, k, j])

    def tower_spread():
        here = tower_slot(d)
        send(here, here, t_plane_send.at[0], t_plane_recv.at[0], chip_x * 2 + c, m)
        send(here, here, t_plane_send.at[1], t_plane_recv.at[1], chip_y * 2 + c, m)
        send(here, here, t_plane_send.at[2], t_plane_recv.at[2], partner, m)

    def tower_relay():
        for j in range(2):
            here = tower_slot(chips[j] * 2 + c)
            arrived(here, t_plane_send.at[j], t_plane_recv.at[j])
            half = tower_slot(chips[j] * 2 + c, j)
            send(half, half, t_diag_send.at[j], t_diag_recv.at[j], chips[1 - j] * 2 + c, m)
            send(here, here, t_pair_send.at[j], t_pair_recv.at[j], partner, m)

    def tower_diag():
        for j in range(2):
            half = tower_slot(chip_z * 2 + c, j)
            arrived(half, t_diag_send.at[j], t_diag_recv.at[j])
        here = tower_slot(chip_z * 2 + c)
        send(here, here, t_pair_send.at[2], t_pair_recv.at[2], partner, m)

    def tower_complete():
        arrived(tower_slot(partner), t_plane_send.at[2], t_plane_recv.at[2])
        for j in range(3):
            here = tower_slot(chips[j] * 2 + 1 - c)
            arrived(here, t_pair_send.at[j], t_pair_recv.at[j])

    step = 16 if rows % 16 == 0 else 8

    def pool(group):
        first = pl.multiple_of((group * members + m) * rows, rows)

        def some(index, carry):
            base = pl.multiple_of(index * step, step)
            for r in range(step):
                total = None
                for hot in range(hots):
                    at = ids[hot, first + base + r]
                    row = table_wide[pl.ds(at, 1), :]
                    total = row if total is None else total + row
                sums[pl.ds(base + r, 1), :] = total
            return carry

        lax.fori_loop(0, rows // step, some, 0)
        return sums[...].astype(jnp.bfloat16)

    def pool_out(i):
        outbox[i] = pool(wrap(d + i, groups))

    def pool_away(i):
        to = wrap(d + i, groups)
        send(outbox.at[i], pooled.at[d], pool_send.at[i], pool_recv.at[i], to, m)

    table_copy.wait()
    table_wide[...] = table_half[...].astype(jnp.float32)
    ids_copy.wait()
    early = 2
    for i in range(1, early + 1):
        pool_out(i)
    pl.semaphore_wait(barrier, members - 1 + groups - 1)

    for p in range(pieces):
        for k in range(1, members):
            own = pl.ds(pl.multiple_of(d * piece, piece), piece)
            send(
                source(p).at[own, :],
                slot(p, m, d),
                z_send.at[p, k],
                z_recv.at[p, k],
                d,
                goes(k),
            )
        if p == 0:
            for k in range(1, members):
                send(bias, biases.at[m], bias_send.at[k], bias_recv.at[k], d, goes(k))
    for i in range(1, groups):
        if i > early:
            pool_out(i)
        pool_away(i)
    pooled[d] = pool(d)

    spread(0)
    spread(1)
    relay(0)
    order_copy.wait()
    for i in range(1, groups):
        arrived(pooled.at[wrap(d - i, groups)], pool_send.at[i], pool_recv.at[i])
    per_block = block // embed
    for b in range(members):
        features = [pooled[order[b * per_block + f]] for f in range(per_block)]
        embedded[b] = jnp.concatenate(features, axis=1)
    bias_copy.wait()
    for k in range(1, members):
        arrived(biases.at[came(k)], bias_send.at[k], bias_recv.at[k])
    for p in range(2, pieces):
        spread(p)
        relay(p - 1)
        diag(p - 2)
    relay(pieces - 1)
    tower_copy.wait()
    tower_spread()
    diag(pieces - 2)

    def matching(p, b):
        return weights[p, pl.ds(pl.multiple_of(b * block, block), block), :]

    for layer in range(layers):
        p = 2 * layer
        last = layer == layers - 1
        state = embedded if layer == 0 else crossed
        projected = None
        for k in range(members):
            complete(p, k)
            b = came(k)
            term = jnp.dot(state[b], matching(p, b), preferred_element_type=jnp.float32)
            projected = term if projected is None else projected + term
        projected = projected.astype(jnp.bfloat16)
        for k in range(members):
            if last and k + 1 < members:
                finish_diag(p + 1, k + 1)
            complete(p + 1, k)
            b = came(k)
            lifted = lax.dot_general(
                projected,
                matching(p + 1, b),
                (((1,), (1,)), ((), ())),
                preferred_element_type=jnp.float32,
            )
            wide = embedded[b].astype(jnp.float32)
            value = wide * (lifted + biases[b, layer : layer + 1, :]) + state[b].astype(jnp.float32)
            value = value.astype(jnp.bfloat16)
            if not last:
                crossed[b] = value
                continue
            crossed_all[m, b] = value
            for to in range(1, members):
                send(
                    crossed_all.at[m, b],
                    crossed_all.at[m, b],
                    cross_send.at[k, to],
                    cross_recv.at[k, to],
                    d,
                    goes(to),
                )

    tower_relay()
    tower_diag()
    tower_bias_copy.wait()
    tower_complete()

    def finish(member):
        value = None
        for b in range(members):
            part = jnp.dot(
                crossed_all[member, b],
                tower_all[b * block : (b + 1) * block, :],
                preferred_element_type=jnp.float32,
            )
            value = part if value is None else value + part
        value = jnp.maximum(value + tower_bias[...], 0.0).astype(jnp.bfloat16)
        out[pl.ds(pl.multiple_of(member * rows, rows), rows), :] = value

    finish(m)
    for to in sorted(range(1, members), key=lambda k: min(k, members - k)):
        sender = came(to)
        for k in range(members):
            here = crossed_all.at[sender, wrap(sender - k, members)]
            arrived(here, cross_send.at[k, to], cross_recv.at[k, to])
        finish(sender)
    for copy in sends:
        copy.wait_send()


def fused_body(
    feature_ids,
    tables,
    table_of_feature,
    cross_down,
    cross_up,
    cross_bias,
    tower_weight,
    tower_bias,
):
    groups = lax.axis_size("dp")
    members = lax.axis_size("mp")
    _, batch_size, hot_count = feature_ids.shape
    rows = batch_size // (groups * members)
    _, vocab, embed = tables.shape
    layers, block, rank = cross_down.shape
    depth, units = tower_weight.shape
    width = block * members
    pieces = 2 * layers
    dma = pltpu.SemaphoreType.DMA
    anywhere = pl.BlockSpec(memory_space=pl.ANY)
    vmem = pl.BlockSpec(memory_space=pltpu.VMEM)
    return pl.pallas_call(
        functools.partial(kernel, groups, members),
        out_shape=pltpu.VMEM((rows * members, units), jnp.bfloat16),
        in_specs=[anywhere] * 8,
        out_specs=vmem,
        scratch_shapes=[
            pltpu.SMEM((hot_count, batch_size), jnp.int32),
            pltpu.SMEM(table_of_feature.shape, jnp.int32),
            pltpu.VMEM((vocab, embed), jnp.bfloat16),
            pltpu.VMEM((vocab, embed), jnp.float32),
            pltpu.VMEM((rows, embed), jnp.float32),
            pltpu.VMEM((groups, rows, embed), jnp.bfloat16),
            pltpu.VMEM((groups, rows, embed), jnp.bfloat16),
            pltpu.VMEM((members, rows, block), jnp.bfloat16),
            pltpu.VMEM((members, rows, block), jnp.bfloat16),
            pltpu.VMEM((pieces, width, rank), jnp.bfloat16),
            pltpu.VMEM((members, layers, block), jnp.float32),
            pltpu.VMEM((width, units), jnp.bfloat16),
            pltpu.VMEM((1, units), jnp.float32),
            pltpu.VMEM((members, members, rows, block), jnp.bfloat16),
            dma((6 + pieces,)),
            dma((pieces, members)),
            dma((pieces, members)),
            dma((pieces, members, 3)),
            dma((pieces, members, 3)),
            dma((pieces, members, 2)),
            dma((pieces, members, 2)),
            dma((pieces, members, 3)),
            dma((pieces, members, 3)),
            dma((members,)),
            dma((members,)),
            dma((3,)),
            dma((3,)),
            dma((2,)),
            dma((2,)),
            dma((3,)),
            dma((3,)),
            dma((groups,)),
            dma((groups,)),
            dma((members, members)),
            dma((members, members)),
        ],
        compiler_params=pltpu.CompilerParams(
            collective_id=0, has_side_effects=True, vmem_limit_bytes=VMEM_BYTES
        ),
    )(
        feature_ids[0].T,
        table_of_feature,
        tables,
        cross_down,
        cross_up,
        cross_bias,
        tower_weight,
        tower_bias.reshape(1, -1),
    )


def body(
    feature_ids,
    tables,
    table_of_feature,
    cross_down,
    cross_up,
    cross_bias,
    tower_weight,
    tower_bias,
):
    groups = lax.axis_size("dp")
    members = lax.axis_size("mp")
    held = 2 * members * (cross_down.size + cross_up.size) + 2 * groups * tower_weight.size
    fits = held <= KERNEL_BYTES and groups == 2 * CHIPS and tables.shape[0] == 1
    chosen = fused_body if fits else plain_body
    return chosen(
        feature_ids,
        tables,
        table_of_feature,
        cross_down,
        cross_up,
        cross_bias,
        tower_weight,
        tower_bias,
    )


def solution(mesh):
    return jax.shard_map(
        body,
        mesh=mesh,
        in_specs=(
            P("dp", None, None),
            P("dp", None, None),
            P(),
            P(None, "mp", None),
            P(None, "mp", None),
            P(None, "mp"),
            P("dp", "mp"),
            P("mp"),
        ),
        out_specs=P("dp", "mp"),
        check_vma=False,
    )
```

profile of v0, /device:TPU:0, one launch (start us, length us, event | category | flops | bytes accessed | tf_op | source)
XLA Modules:
  0.0 45.2 jit_solution(7961983364393673256)
XLA Ops:
  0.0 44.5 %shard_map.82 = bf16[256,512]{1,0:T(8,128)(2,1)S(1)} custom-call(s32[8,2048]{1,0:T(8,128)} %bitcast.4, s32[8]{0:T(128)} %order_hbm.1, bf16[1,4096,128]{2,1,0:T(8,128)(2,1)} %table.1, bf16[2,256,512]{2,1,0:T(8,128)(2,1)} %down.1, bf16[2,256,512]{2,1,0:T(8,128)(2,1)} %up.1, f32[2,256]{1,0:T(2,128)} %bias.1, bf16[128,512]{1,0:T(8,128)(2,1)} %tower.1, ...), custom_call_target="tpu_custom_call" | custom-call | tf_op jit(solution)/shard_map/pallas_call | solution.py:446
  44.5 0.7 %copy.10 = bf16[256,512]{1,0:T(8,128)(2,1)} copy(bf16[256,512]{1,0:T(8,128)(2,1)S(1)} %shard_map.82) | data formatting | bytes 524288
where the time goes:
time: 45.4 us; the launch traced here: 45.2 us
  Pallas kernels  44.5 us (98%)
  local copies, waits for them, and re-layouts  0.71 us (2%)
    pallas_call x1, Pallas kernels, fused_body(): pl.pallas_call(functools.partial(kernel, groups, members), out_shape=pltp...  44.5 us

commit v1 on v0

v1 whole, which is shorter than its diff:
```python
import functools

import jax
import jax.numpy as jnp
from jax import lax
from jax.experimental import pallas as pl
from jax.experimental.pallas import tpu as pltpu
from jax.sharding import PartitionSpec as P


def plain_body(
    feature_ids,
    tables,
    table_of_feature,
    cross_down,
    cross_up,
    cross_bias,
    tower_weight,
    tower_bias,
):
    groups = lax.axis_size("dp")
    members = lax.axis_size("mp")
    member = lax.axis_index("mp")
    table_count, batch_size, hot_count = feature_ids.shape
    row_count = batch_size // (groups * members)
    shaped = feature_ids[0].reshape(groups, members, row_count, hot_count)
    own_ids = lax.dynamic_index_in_dim(shaped, member, 1, keepdims=False).reshape(
        groups * row_count, hot_count
    )
    summed = jnp.zeros((groups * row_count, tables.shape[2]), jnp.float32)
    for hot_index in range(hot_count):
        summed = summed + jnp.take(tables[0], own_ids[:, hot_index], axis=0).astype(jnp.float32)
    columns = [summed.astype(jnp.bfloat16)]
    pooled = jnp.stack(columns, axis=1)
    regrouped = lax.all_to_all(pooled, "dp", split_axis=0, concat_axis=1, tiled=True)
    ordered = jnp.take(regrouped, table_of_feature, axis=1)
    by_width = lax.all_to_all(ordered, "mp", split_axis=1, concat_axis=0, tiled=True)
    group_rows = by_width.shape[0]
    embedded = by_width.reshape(group_rows, -1)
    embedded_wide = embedded.astype(jnp.float32)
    crossed = embedded
    layer_total = cross_down.shape[0]
    for layer_index in range(layer_total):
        partial_value = jnp.dot(
            crossed, cross_down[layer_index], preferred_element_type=jnp.float32
        )
        projected = lax.psum(partial_value.astype(jnp.bfloat16), "mp")
        lifted = lax.dot_general(
            projected,
            cross_up[layer_index],
            (((1,), (1,)), ((), ())),
            preferred_element_type=jnp.float32,
        )
        crossed = (
            embedded_wide * (lifted + cross_bias[layer_index]) + crossed.astype(jnp.float32)
        ).astype(jnp.bfloat16)
    full_rows = lax.all_gather(crossed, "mp", axis=1, tiled=True)
    pre_act = jnp.dot(
        full_rows,
        lax.all_gather(tower_weight, "dp", axis=0, tiled=True),
        preferred_element_type=jnp.float32,
    )
    return jax.nn.relu(pre_act + tower_bias).astype(jnp.bfloat16)


MESH = pl.DeviceIdType.MESH
KERNEL_BYTES = 24 * 1024 * 1024
VMEM_BYTES = (64 * 1024 - 352) * 1024
CHIPS = 4
PLANES = 4
STEPS = (1, 3, 2)


def kernel(
    groups,
    members,
    ids_hbm,
    order_hbm,
    table,
    down,
    up,
    bias,
    tower,
    tower_bias_hbm,
    out,
    ids,
    order,
    table_half,
    table_wide,
    sums,
    outbox,
    pooled,
    embedded,
    crossed,
    weights,
    biases,
    tower_all,
    tower_bias,
    local_sem,
    send_sem,
    z_recv,
    plane_recv,
    diag_recv,
    pair_recv,
    tower_recv,
    pool_recv,
    share_recv,
    bias_recv,
):
    d = lax.axis_index("dp")
    m = lax.axis_index("mp")
    q = lax.div(d, 2)
    c = lax.rem(d, 2)
    partner = q * 2 + 1 - c
    chip_x = q + 1 - 2 * lax.rem(q, 2)
    chip_y = lax.rem(q + 2, CHIPS)
    chip_z = lax.rem(chip_x + 2, CHIPS)
    chips = (chip_x, chip_y, chip_z)
    layers, block, rank = down.shape
    hots = ids.shape[0]
    rows, embed = sums.shape
    piece = block // groups
    depth = tower.shape[0]
    pieces = 2 * layers
    others = members - 1

    def wrap(value, size):
        return lax.rem(value + size, size)

    def load(src, dst, index):
        copy = pltpu.make_async_copy(src, dst, local_sem.at[index])
        copy.start()
        return copy

    def remote(src, dst, which, recv_sem, to_d, to_m):
        return pltpu.make_async_remote_copy(
            src_ref=src,
            dst_ref=dst,
            send_sem=send_sem.at[which],
            recv_sem=recv_sem,
            device_id=(to_d, to_m),
            device_id_type=MESH,
        )

    def send(src, dst, which, recv_sem, to_d, to_m):
        remote(src, dst, which, recv_sem, to_d, to_m).start()

    def arrived(ref, recv_sem):
        remote(ref, ref, 0, recv_sem, partner, m).wait_recv()

    def came(k):
        return wrap(m - k, members)

    def goes(k):
        return wrap(m + k, members)

    def slot(p, member, device, half=None):
        length = piece if half is None else piece // 2
        start = member * block + device * piece + (0 if half is None else half * length)
        return weights.at[p, pl.ds(pl.multiple_of(start, length), length), :]

    def tower_slot(device, half=None):
        length = depth if half is None else depth // 2
        start = device * depth + (0 if half is None else half * length)
        return tower_all.at[pl.ds(pl.multiple_of(start, length), length), :]

    def source(p):
        return (down, up)[p % 2].at[p // 2]

    barrier = pltpu.get_barrier_semaphore()
    for k in range(1, members):
        pl.semaphore_signal(barrier, inc=1, device_id=(d, goes(k)), device_id_type=MESH)
    for i in range(1, groups):
        pl.semaphore_signal(barrier, inc=1, device_id=(wrap(d + i, groups), m), device_id_type=MESH)

    here = pl.ds(pl.multiple_of(m * block, block), block)
    own = pl.ds(pl.multiple_of(d * piece, piece), piece)
    tower_copy = load(tower, tower_slot(d), 0)
    weight_copies = [load(source(p), weights.at[p, here, :], 1 + p) for p in range(pieces)]
    table_copy = load(table.at[0], table_half, pieces + 1)
    ids_copy = load(ids_hbm, ids, pieces + 2)
    bias_copy = load(bias, biases.at[m], pieces + 3)
    order_copy = load(order_hbm, order, pieces + 4)
    tower_bias_copy = load(tower_bias_hbm, tower_bias, pieces + 5)

    def lend(p):
        for k in STEPS:
            mine = slot(p, m, d)
            send(mine, mine, 0, z_recv.at[p, k - 1], d, goes(k))

    def spread(p, k):
        mine = slot(p, came(k), d)
        arrived(mine, z_recv.at[p, k - 1])
        send(mine, mine, 0, plane_recv.at[p, k - 1], chip_x * 2 + c, m)
        send(mine, mine, 0, plane_recv.at[p, k - 1], chip_y * 2 + c, m)
        send(mine, mine, 0, pair_recv.at[p, k - 1], partner, m)

    def relay(p, k):
        arrived(weights.at[p, pl.ds(0, 2 * piece), :], plane_recv.at[p, k - 1])
        for j in range(2):
            half = slot(p, came(k), chips[j] * 2 + c, j)
            send(half, half, 0, diag_recv.at[p, k - 1], chips[1 - j] * 2 + c, m)
        for j in range(2):
            whole = slot(p, came(k), chips[j] * 2 + c)
            send(whole, whole, 0, pair_recv.at[p, k - 1], partner, m)

    def corner(p, k):
        far = slot(p, came(k), chip_z * 2 + c)
        arrived(far, diag_recv.at[p, k - 1])
        send(far, far, 0, pair_recv.at[p, k - 1], partner, m)

    def complete(p, k):
        arrived(weights.at[p, pl.ds(0, CHIPS * piece), :], pair_recv.at[p, k - 1])

    def tower_spread():
        mine = tower_slot(d)
        send(mine, mine, 1, tower_recv.at[0], chip_x * 2 + c, m)
        send(mine, mine, 1, tower_recv.at[0], chip_y * 2 + c, m)
        send(mine, mine, 1, tower_recv.at[2], partner, m)

    def tower_relay():
        arrived(tower_all.at[pl.ds(0, 2 * depth), :], tower_recv.at[0])
        for j in range(2):
            half = tower_slot(chips[j] * 2 + c, j)
            send(half, half, 1, tower_recv.at[1], chips[1 - j] * 2 + c, m)
        for j in range(2):
            whole = tower_slot(chips[j] * 2 + c)
            send(whole, whole, 1, tower_recv.at[2], partner, m)

    def tower_corner():
        far = tower_slot(chip_z * 2 + c)
        arrived(far, tower_recv.at[1])
        send(far, far, 1, tower_recv.at[2], partner, m)

    step = 16 if rows % 16 == 0 else 8

    def pool(group):
        first = pl.multiple_of((group * members + m) * rows, rows)

        def some(index, carry):
            base = pl.multiple_of(index * step, step)
            for r in range(step):
                total = None
                for hot in range(hots):
                    at = ids[hot, first + base + r]
                    row = table_wide[pl.ds(at, 1), :]
                    total = row if total is None else total + row
                sums[pl.ds(base + r, 1), :] = total
            return carry

        lax.fori_loop(0, rows // step, some, 0)
        return sums[...].astype(jnp.bfloat16)

    def pool_out(i):
        if i == 0:
            pooled[m, d] = pool(d)
        else:
            outbox[i] = pool(wrap(d + i, groups))

    def pool_away(i):
        send(outbox.at[i], pooled.at[m, d], 2, pool_recv.at[0], wrap(d + i, groups), m)

    half_of = lax.div(m, 2)
    beside = m + 1 - 2 * lax.rem(m, 2)
    across = 2 - half_of
    far_first = 2 * (1 - half_of)
    inner = jnp.logical_or(m == 1, m == 2)

    def share():
        arrived(outbox.at[pl.ds(0, groups - 1)], pool_recv.at[0])
        mine = pooled.at[m]
        send(mine, mine, 3, share_recv.at[m], d, across)
        send(mine, mine, 3, share_recv.at[m], d, beside)

    def pass_on():
        @pl.when(inner)
        def _():
            for quarter in (3 - m, m + 2 - 4 * half_of):
                theirs = pooled.at[quarter]
                arrived(theirs, share_recv.at[quarter])
                send(theirs, theirs, 3, share_recv.at[quarter], d, beside)

    def shared():
        arrived(pooled.at[beside], share_recv.at[beside])

        @pl.when(jnp.logical_not(inner))
        def _():
            for j in range(2):
                arrived(pooled.at[far_first + j], share_recv.at[far_first + j])

    def matching(p, b):
        return weights[p, pl.ds(pl.multiple_of(b * block, block), block), :]

    def embed_all():
        per_block = block // embed
        order_copy.wait()
        for b in range(members):
            for f in range(per_block):
                at = order[b * per_block + f]
                for quarter in range(members):
                    embedded[
                        b, quarter * rows : (quarter + 1) * rows, f * embed : (f + 1) * embed
                    ] = pooled[quarter, at]

    def project(layer):
        state = embedded if layer == 0 else crossed
        for k in STEPS:
            complete(2 * layer, k)
        value = None
        for b in range(members):
            term = jnp.dot(
                state[b],
                weights[2 * layer, b * block : (b + 1) * block, :],
                preferred_element_type=jnp.float32,
            )
            value = term if value is None else value + term
        return value.astype(jnp.bfloat16)

    def lift(layer, projected, b):
        state = embedded if layer == 0 else crossed
        lifted = lax.dot_general(
            projected,
            matching(2 * layer + 1, b),
            (((1,), (1,)), ((), ())),
            preferred_element_type=jnp.float32,
        )
        wide = embedded[b].astype(jnp.float32)
        value = wide * (lifted + biases[b, layer : layer + 1, :]) + state[b].astype(jnp.float32)
        return value.astype(jnp.bfloat16)

    units = [(p, k) for p in range(pieces) for k in STEPS]

    def at_scope(name, call, *args):
        with jax.named_scope(name):
            return call(*args)

    def do(call, *args):
        return at_scope(call.__name__ + "_".join(map(str, args)), call, *args)

    def first_sends():
        tower_copy.wait()
        for copy in weight_copies:
            copy.wait()
        bias_copy.wait()
        pl.semaphore_wait(barrier, members - 1 + groups - 1)

    do(first_sends)
    tower_spread()
    lend(0)
    for k in range(1, members):
        send(biases.at[m], biases.at[m], 4, bias_recv.at[0], d, goes(k))
    lend(1)

    def widen():
        table_copy.wait()
        table_wide[...] = table_half[...].astype(jnp.float32)
        ids_copy.wait()

    do(widen)
    jobs = {
        3: [(spread, *units[0])],
        4: [(spread, *units[1])],
        5: [(spread, *units[2]), (tower_relay,)],
        6: [(relay, *units[0]), (spread, *units[3])],
        7: [(relay, *units[1]), (spread, *units[4])],
        8: [(tower_corner,), (relay, *units[2])],
    }
    for turn in range(1, groups + 1):
        i = turn % groups
        do(pool_out, i)
        if turn > 1:
            pool_away(turn - 1)
        for job in jobs.get(turn, []):
            do(*job)
    do(share)
    lend(2)
    lend(3)
    spread_done, relay_done, corner_done = 5, 3, 0

    def upto(kind, done, count):
        for unit in units[done:count]:
            do(kind, *unit)
        return count

    def advance(target):
        nonlocal spread_done, relay_done, corner_done
        while spread_done < min(target, len(units)):
            spread_done = upto(spread, spread_done, spread_done + 1)
            relay_done = upto(relay, relay_done, max(relay_done, spread_done - 2))
            corner_done = upto(corner, corner_done, max(corner_done, spread_done - 4))

    advance(7)
    do(pass_on)
    advance(9)
    do(shared)
    do(embed_all)
    corner_done = upto(corner, corner_done, max(corner_done, 3))
    arrived(biases.at[pl.ds(0, others)], bias_recv.at[0])
    projected = do(project, 0)
    advance(11)
    corner_done = upto(corner, corner_done, max(corner_done, 6))
    for k in (0,) + STEPS:
        if k:
            do(complete, 1, k)
        b = came(k)
        crossed[b] = lift(0, projected, b)
    advance(12)
    relay_done = upto(relay, relay_done, 11)
    corner_done = upto(corner, corner_done, 9)
    projected = do(project, 1)
    relay_done = upto(relay, relay_done, 12)
    tower_bias_copy.wait()
    arrived(tower_all.at[pl.ds(0, CHIPS * depth), :], tower_recv.at[2])
    answer = None
    for k in (0,) + STEPS:
        if k:
            do(corner, pieces - 1, k)
            do(complete, pieces - 1, k)
        b = came(k)
        value = lift(1, projected, b)
        part = jnp.dot(
            value,
            tower_all[pl.ds(pl.multiple_of(b * block, block), block), :],
            preferred_element_type=jnp.float32,
        )
        answer = part if answer is None else answer + part
    out[...] = jnp.maximum(answer + tower_bias[...], 0.0).astype(jnp.bfloat16)

    def sent(ref, which):
        remote(ref, ref, which, bias_recv.at[0], partner, m).wait_send()

    def all_sent():
        sent(weights.at[:, pl.ds(0, others * block), :], 0)
        sent(tower_all.at[pl.ds(0, 7 * depth), :], 1)
        sent(outbox.at[pl.ds(0, groups - 1)], 2)
        sent(pooled.at[pl.ds(0, 2)], 3)

        @pl.when(inner)
        def _():
            sent(pooled.at[pl.ds(0, 2)], 3)

        sent(biases.at[pl.ds(0, others)], 4)

    do(all_sent)


def fused_body(
    feature_ids,
    tables,
    table_of_feature,
    cross_down,
    cross_up,
    cross_bias,
    tower_weight,
    tower_bias,
):
    groups = lax.axis_size("dp")
    members = lax.axis_size("mp")
    _, batch_size, hot_count = feature_ids.shape
    rows = batch_size // (groups * members)
    _, vocab, embed = tables.shape
    layers, block, rank = cross_down.shape
    depth, units = tower_weight.shape
    width = block * members
    pieces = 2 * layers
    dma = pltpu.SemaphoreType.DMA
    anywhere = pl.BlockSpec(memory_space=pl.ANY)
    vmem = pl.BlockSpec(memory_space=pltpu.VMEM)
    return pl.pallas_call(
        functools.partial(kernel, groups, members),
        out_shape=pltpu.VMEM((rows * members, units), jnp.bfloat16),
        in_specs=[anywhere] * 8,
        out_specs=vmem,
        scratch_shapes=[
            pltpu.SMEM((hot_count, batch_size), jnp.int32),
            pltpu.SMEM(table_of_feature.shape, jnp.int32),
            pltpu.VMEM((vocab, embed), jnp.bfloat16),
            pltpu.VMEM((vocab, embed), jnp.float32),
            pltpu.VMEM((rows, embed), jnp.float32),
            pltpu.VMEM((groups, rows, embed), jnp.bfloat16),
            pltpu.VMEM((members, groups, rows, embed), jnp.bfloat16),
            pltpu.VMEM((members, rows * members, block), jnp.bfloat16),
            pltpu.VMEM((members, rows * members, block), jnp.bfloat16),
            pltpu.VMEM((pieces, width, rank), jnp.bfloat16),
            pltpu.VMEM((members, layers, block), jnp.float32),
            pltpu.VMEM((width, units), jnp.bfloat16),
            pltpu.VMEM((1, units), jnp.float32),
            dma((6 + pieces,)),
            dma((5,)),
            dma((pieces, members - 1)),
            dma((pieces, members - 1)),
            dma((pieces, members - 1)),
            dma((pieces, members - 1)),
            dma((3,)),
            dma((1,)),
            dma((members,)),
            dma((1,)),
        ],
        compiler_params=pltpu.CompilerParams(
            collective_id=0, has_side_effects=True, vmem_limit_bytes=VMEM_BYTES
        ),
    )(
        feature_ids[0].T,
        table_of_feature,
        tables,
        cross_down,
        cross_up,
        cross_bias,
        tower_weight,
        tower_bias.reshape(1, -1),
    )


def body(
    feature_ids,
    tables,
    table_of_feature,
    cross_down,
    cross_up,
    cross_bias,
    tower_weight,
    tower_bias,
):
    groups = lax.axis_size("dp")
    members = lax.axis_size("mp")
    held = 2 * members * (cross_down.size + cross_up.size) + 2 * groups * tower_weight.size
    placed = groups == 2 * CHIPS and members == PLANES
    fits = held <= KERNEL_BYTES and placed and tables.shape[0] == 1
    chosen = fused_body if fits else plain_body
    return chosen(
        feature_ids,
        tables,
        table_of_feature,
        cross_down,
        cross_up,
        cross_bias,
        tower_weight,
        tower_bias,
    )


def solution(mesh):
    return jax.shard_map(
        body,
        mesh=mesh,
        in_specs=(
            P("dp", None, None),
            P("dp", None, None),
            P(),
            P(None, "mp", None),
            P(None, "mp", None),
            P(None, "mp"),
            P("dp", "mp"),
            P("mp"),
        ),
        out_specs=P("dp", "mp"),
        check_vma=False,
    )
```

time: 45.4 us -> 46.9 us (1.033)
  Pallas kernels: 44.5 us -> 45.7 us
    pallas_call x1, Pallas kernels: 44.5 us -> 45.7 us  [fused_body(): pl.pallas_call(functools.partial(kernel, groups, members), out_shape=pltp...]
where the time goes in v1:
time: 46.9 us; the launch traced here: 46.4 us
  Pallas kernels  45.7 us (97%)
  local copies, waits for them, and re-layouts  0.71 us (2%)
    pallas_call x1, Pallas kernels, fused_body(): pl.pallas_call(functools.partial(kernel, groups, members), out_shape=pltp...  45.7 us

profile of v1, /device:TPU:0, one launch (start us, length us, event | category | flops | bytes accessed | tf_op | source)
XLA Modules:
  0.0 46.4 jit_solution(15912612115145456013)
XLA Ops:
  0.0 45.7 %shard_map.82 = bf16[256,512]{1,0:T(8,128)(2,1)S(1)} custom-call(s32[8,2048]{1,0:T(8,128)} %bitcast.4, s32[8]{0:T(128)} %order_hbm.1, bf16[1,4096,128]{2,1,0:T(8,128)(2,1)} %table.1, bf16[2,256,512]{2,1,0:T(8,128)(2,1)} %down.1, bf16[2,256,512]{2,1,0:T(8,128)(2,1)} %up.1, f32[2,256]{1,0:T(2,128)} %bias.1, bf16[128,512]{1,0:T(8,128)(2,1)} %tower.1, ...), custom_call_target="tpu_custom_call" | custom-call | tf_op jit(solution)/shard_map/pallas_call | solution.py:469
  45.7 0.7 %copy.10 = bf16[256,512]{1,0:T(8,128)(2,1)} copy(bf16[256,512]{1,0:T(8,128)(2,1)S(1)} %shard_map.82) | data formatting | bytes 524288

commit v2 on v1

--- a/solution.py
+++ b/solution.py
@@ -69,6 +69,13 @@
 CHIPS = 4
 PLANES = 4
 STEPS = (1, 3, 2)
+PLAN = (
+    "flip", "widen", "P1", "P2", "A1", "L1", "P3", "A2", "L3", "P4", "A3", "S0", "S1", "P5",
+    "A4", "P6", "A5", "S2", "P7", "A6", "TR", "P0", "A7", "R0", "R1", "S3", "S4", "R2", "S5",
+    "SH", "R3", "R4", "S6", "R5", "S7", "S8", "C0", "C1", "C2", "TC", "R6", "S9", "R7", "S10",
+    "R8", "S11", "C3", "C4", "C5", "R9", "F1", "R10", "F0", "R11", "C6", "C7", "C8", "E", "X0",
+    "Y", "C9", "C10", "C11", "X1", "Z01", "Z32", "end",
+)
 
 
 def kernel(
@@ -93,6 +100,8 @@
     embedded,
     crossed,
     weights,
+    up_raw,
+    lifts,
     biases,
     tower_all,
     tower_bias,
@@ -154,18 +163,26 @@
     def goes(k):
         return wrap(m + k, members)
 
+    thin = rank // groups
+
     def slot(p, member, device, half=None):
-        length = piece if half is None else piece // 2
-        start = member * block + device * piece + (0 if half is None else half * length)
-        return weights.at[p, pl.ds(pl.multiple_of(start, length), length), :]
+        full = piece if p % 2 == 0 else thin
+        length = full if half is None else full // 2
+        start = device * full + (0 if half is None else half * length)
+        if p % 2 == 0:
+            start = member * block + start
+            return weights.at[p // 2, pl.ds(pl.multiple_of(start, length), length), :]
+        return lifts.at[p // 2, member, pl.ds(pl.multiple_of(start, length), length), :]
+
+    def amount(p, count):
+        if p % 2 == 0:
+            return weights.at[p // 2, pl.ds(0, count * piece), :]
+        return lifts.at[p // 2, 0, pl.ds(0, count * thin), :]
 
     def tower_slot(device, half=None):
         length = depth if half is None else depth // 2
         start = device * depth + (0 if half is None else half * length)
         return tower_all.at[pl.ds(pl.multiple_of(start, length), length), :]
-
-    def source(p):
-        return (down, up)[p % 2].at[p // 2]
 
     barrier = pltpu.get_barrier_semaphore()
     for k in range(1, members):
@@ -174,9 +191,9 @@
         pl.semaphore_signal(barrier, inc=1, device_id=(wrap(d + i, groups), m), device_id_type=MESH)
 
     here = pl.ds(pl.multiple_of(m * block, block), block)
-    own = pl.ds(pl.multiple_of(d * piece, piece), piece)
     tower_copy = load(tower, tower_slot(d), 0)
-    weight_copies = [load(source(p), weights.at[p, here, :], 1 + p) for p in range(pieces)]
+    weight_copies = [load(down.at[n], weights.at[n, here, :], 1 + n) for n in range(layers)]
+    up_copies = [load(up.at[n], up_raw.at[n], 1 + layers + n) for n in range(layers)]
     table_copy = load(table.at[0], table_half, pieces + 1)
     ids_copy = load(ids_hbm, ids, pieces + 2)
     bias_copy = load(bias, biases.at[m], pieces + 3)
@@ -186,51 +203,51 @@
     def lend(p):
         for k in STEPS:
             mine = slot(p, m, d)
-            send(mine, mine, 0, z_recv.at[p, k - 1], d, goes(k))
+            send(mine, mine, p % 2, z_recv.at[p, k - 1], d, goes(k))
 
     def spread(p, k):
         mine = slot(p, came(k), d)
         arrived(mine, z_recv.at[p, k - 1])
-        send(mine, mine, 0, plane_recv.at[p, k - 1], chip_x * 2 + c, m)
-        send(mine, mine, 0, plane_recv.at[p, k - 1], chip_y * 2 + c, m)
-        send(mine, mine, 0, pair_recv.at[p, k - 1], partner, m)
+        send(mine, mine, p % 2, plane_recv.at[p, k - 1], chip_x * 2 + c, m)
+        send(mine, mine, p % 2, plane_recv.at[p, k - 1], chip_y * 2 + c, m)
+        send(mine, mine, p % 2, pair_recv.at[p, k - 1], partner, m)
 
     def relay(p, k):
-        arrived(weights.at[p, pl.ds(0, 2 * piece), :], plane_recv.at[p, k - 1])
+        arrived(amount(p, 2), plane_recv.at[p, k - 1])
         for j in range(2):
             half = slot(p, came(k), chips[j] * 2 + c, j)
-            send(half, half, 0, diag_recv.at[p, k - 1], chips[1 - j] * 2 + c, m)
+            send(half, half, p % 2, diag_recv.at[p, k - 1], chips[1 - j] * 2 + c, m)
         for j in range(2):
             whole = slot(p, came(k), chips[j] * 2 + c)
-            send(whole, whole, 0, pair_recv.at[p, k - 1], partner, m)
+            send(whole, whole, p % 2, pair_recv.at[p, k - 1], partner, m)
 
     def corner(p, k):
         far = slot(p, came(k), chip_z * 2 + c)
         arrived(far, diag_recv.at[p, k - 1])
-        send(far, far, 0, pair_recv.at[p, k - 1], partner, m)
+        send(far, far, p % 2, pair_recv.at[p, k - 1], partner, m)
 
     def complete(p, k):
-        arrived(weights.at[p, pl.ds(0, CHIPS * piece), :], pair_recv.at[p, k - 1])
+        arrived(amount(p, CHIPS), pair_recv.at[p, k - 1])
 
     def tower_spread():
         mine = tower_slot(d)
-        send(mine, mine, 1, tower_recv.at[0], chip_x * 2 + c, m)
-        send(mine, mine, 1, tower_recv.at[0], chip_y * 2 + c, m)
-        send(mine, mine, 1, tower_recv.at[2], partner, m)
+        send(mine, mine, 2, tower_recv.at[0], chip_x * 2 + c, m)
+        send(mine, mine, 2, tower_recv.at[0], chip_y * 2 + c, m)
+        send(mine, mine, 2, tower_recv.at[2], partner, m)
 
     def tower_relay():
         arrived(tower_all.at[pl.ds(0, 2 * depth), :], tower_recv.at[0])
         for j in range(2):
             half = tower_slot(chips[j] * 2 + c, j)
-            send(half, half, 1, tower_recv.at[1], chips[1 - j] * 2 + c, m)
+            send(half, half, 2, tower_recv.at[1], chips[1 - j] * 2 + c, m)
         for j in range(2):
             whole = tower_slot(chips[j] * 2 + c)
-            send(whole, whole, 1, tower_recv.at[2], partner, m)
+            send(whole, whole, 2, tower_recv.at[2], partner, m)
 
     def tower_corner():
         far = tower_slot(chip_z * 2 + c)
         arrived(far, tower_recv.at[1])
-        send(far, far, 1, tower_recv.at[2], partner, m)
+        send(far, far, 2, tower_recv.at[2], partner, m)
 
     step = 16 if rows % 16 == 0 else 8
 
@@ -258,7 +275,7 @@
             outbox[i] = pool(wrap(d + i, groups))
 
     def pool_away(i):
-        send(outbox.at[i], pooled.at[m, d], 2, pool_recv.at[0], wrap(d + i, groups), m)
+        send(outbox.at[i], pooled.at[m, d], 3, pool_recv.at[0], wrap(d + i, groups), m)
 
     half_of = lax.div(m, 2)
     beside = m + 1 - 2 * lax.rem(m, 2)
@@ -269,16 +286,17 @@
     def share():
         arrived(outbox.at[pl.ds(0, groups - 1)], pool_recv.at[0])
         mine = pooled.at[m]
-        send(mine, mine, 3, share_recv.at[m], d, across)
-        send(mine, mine, 3, share_recv.at[m], d, beside)
-
-    def pass_on():
+        send(mine, mine, 4, share_recv.at[m], d, across)
+        send(mine, mine, 4, share_recv.at[m], d, beside)
+
+    def pass_on(far):
+        quarter = m + 2 - 4 * half_of if far else 3 - m
+
         @pl.when(inner)
         def _():
-            for quarter in (3 - m, m + 2 - 4 * half_of):
-                theirs = pooled.at[quarter]
-                arrived(theirs, share_recv.at[quarter])
-                send(theirs, theirs, 3, share_recv.at[quarter], d, beside)
+            theirs = pooled.at[quarter]
+            arrived(theirs, share_recv.at[quarter])
+            send(theirs, theirs, 4, share_recv.at[quarter], d, beside)
 
     def shared():
         arrived(pooled.at[beside], share_recv.at[beside])
@@ -287,9 +305,6 @@
         def _():
             for j in range(2):
                 arrived(pooled.at[far_first + j], share_recv.at[far_first + j])
-
-    def matching(p, b):
-        return weights[p, pl.ds(pl.multiple_of(b * block, block), block), :]
 
     def embed_all():
         per_block = block // embed
@@ -304,13 +319,11 @@
 
     def project(layer):
         state = embedded if layer == 0 else crossed
-        for k in STEPS:
-            complete(2 * layer, k)
         value = None
         for b in range(members):
             term = jnp.dot(
                 state[b],
-                weights[2 * layer, b * block : (b + 1) * block, :],
+                weights[layer, b * block : (b + 1) * block, :],
                 preferred_element_type=jnp.float32,
             )
             value = term if value is None else value + term
@@ -318,24 +331,17 @@
 
     def lift(layer, projected, b):
         state = embedded if layer == 0 else crossed
-        lifted = lax.dot_general(
-            projected,
-            matching(2 * layer + 1, b),
-            (((1,), (1,)), ((), ())),
-            preferred_element_type=jnp.float32,
-        )
+        lifted = jnp.dot(projected, lifts[layer, b], preferred_element_type=jnp.float32)
         wide = embedded[b].astype(jnp.float32)
         value = wide * (lifted + biases[b, layer : layer + 1, :]) + state[b].astype(jnp.float32)
         return value.astype(jnp.bfloat16)
 
-    units = [(p, k) for p in range(pieces) for k in STEPS]
-
-    def at_scope(name, call, *args):
-        with jax.named_scope(name):
+    order_of = tuple(range(0, pieces - 1, 2)) + tuple(range(1, pieces, 2))
+    units = [(p, k) for p in order_of for k in STEPS]
+
+    def do(call, *args):
+        with jax.named_scope(call.__name__ + "_".join(map(str, args))):
             return call(*args)
-
-    def do(call, *args):
-        return at_scope(call.__name__ + "_".join(map(str, args)), call, *args)
 
     def first_sends():
         tower_copy.wait()
@@ -343,104 +349,105 @@
             copy.wait()
         bias_copy.wait()
         pl.semaphore_wait(barrier, members - 1 + groups - 1)
-
-    do(first_sends)
-    tower_spread()
-    lend(0)
-    for k in range(1, members):
-        send(biases.at[m], biases.at[m], 4, bias_recv.at[0], d, goes(k))
-    lend(1)
+        tower_spread()
+        lend(0)
+        for k in range(1, members):
+            send(biases.at[m], biases.at[m], 5, bias_recv.at[0], d, goes(k))
+        lend(2)
+
+    def flip():
+        for n in range(layers):
+            up_copies[n].wait()
+            lifts[n, m] = up_raw[n].T
 
     def widen():
         table_copy.wait()
         table_wide[...] = table_half[...].astype(jnp.float32)
         ids_copy.wait()
 
-    do(widen)
-    jobs = {
-        3: [(spread, *units[0])],
-        4: [(spread, *units[1])],
-        5: [(spread, *units[2]), (tower_relay,)],
-        6: [(relay, *units[0]), (spread, *units[3])],
-        7: [(relay, *units[1]), (spread, *units[4])],
-        8: [(tower_corner,), (relay, *units[2])],
-    }
-    for turn in range(1, groups + 1):
-        i = turn % groups
-        do(pool_out, i)
-        if turn > 1:
-            pool_away(turn - 1)
-        for job in jobs.get(turn, []):
-            do(*job)
-    do(share)
-    lend(2)
-    lend(3)
-    spread_done, relay_done, corner_done = 5, 3, 0
-
-    def upto(kind, done, count):
-        for unit in units[done:count]:
-            do(kind, *unit)
-        return count
-
-    def advance(target):
-        nonlocal spread_done, relay_done, corner_done
-        while spread_done < min(target, len(units)):
-            spread_done = upto(spread, spread_done, spread_done + 1)
-            relay_done = upto(relay, relay_done, max(relay_done, spread_done - 2))
-            corner_done = upto(corner, corner_done, max(corner_done, spread_done - 4))
-
-    advance(7)
-    do(pass_on)
-    advance(9)
-    do(shared)
-    do(embed_all)
-    corner_done = upto(corner, corner_done, max(corner_done, 3))
-    arrived(biases.at[pl.ds(0, others)], bias_recv.at[0])
-    projected = do(project, 0)
-    advance(11)
-    corner_done = upto(corner, corner_done, max(corner_done, 6))
-    for k in (0,) + STEPS:
-        if k:
-            do(complete, 1, k)
-        b = came(k)
-        crossed[b] = lift(0, projected, b)
-    advance(12)
-    relay_done = upto(relay, relay_done, 11)
-    corner_done = upto(corner, corner_done, 9)
-    projected = do(project, 1)
-    relay_done = upto(relay, relay_done, 12)
-    tower_bias_copy.wait()
-    arrived(tower_all.at[pl.ds(0, CHIPS * depth), :], tower_recv.at[2])
-    answer = None
-    for k in (0,) + STEPS:
-        if k:
-            do(corner, pieces - 1, k)
-            do(complete, pieces - 1, k)
-        b = came(k)
-        value = lift(1, projected, b)
-        part = jnp.dot(
-            value,
-            tower_all[pl.ds(pl.multiple_of(b * block, block), block), :],
-            preferred_element_type=jnp.float32,
-        )
-        answer = part if answer is None else answer + part
-    out[...] = jnp.maximum(answer + tower_bias[...], 0.0).astype(jnp.bfloat16)
+    state = {}
+
+    def ready():
+        shared()
+        embed_all()
+        arrived(biases.at[pl.ds(0, others)], bias_recv.at[0])
+
+    def narrow(layer):
+        for k in STEPS:
+            complete(2 * layer, k)
+        state["projected"] = project(layer)
+
+    def lift_first():
+        for k in STEPS:
+            complete(1, k)
+        for b in range(members):
+            crossed[b] = lift(0, state["projected"], b)
+
+    def lift_last(*steps):
+        for k in steps:
+            if k:
+                complete(pieces - 1, k)
+            else:
+                tower_bias_copy.wait()
+                arrived(tower_all.at[pl.ds(0, CHIPS * depth), :], tower_recv.at[2])
+        for k in steps:
+            b = came(k)
+            value = lift(layers - 1, state["projected"], b)
+            part = jnp.dot(
+                value,
+                tower_all[pl.ds(pl.multiple_of(b * block, block), block), :],
+                preferred_element_type=jnp.float32,
+            )
+            state["answer"] = state["answer"] + part if "answer" in state else part
+
+    def finish():
+        total = state["answer"] + tower_bias[...]
+        out[...] = jnp.maximum(total, 0.0).astype(jnp.bfloat16)
 
     def sent(ref, which):
         remote(ref, ref, which, bias_recv.at[0], partner, m).wait_send()
 
     def all_sent():
         sent(weights.at[:, pl.ds(0, others * block), :], 0)
-        sent(tower_all.at[pl.ds(0, 7 * depth), :], 1)
-        sent(outbox.at[pl.ds(0, groups - 1)], 2)
-        sent(pooled.at[pl.ds(0, 2)], 3)
+        sent(lifts.at[:, pl.ds(0, others)], 1)
+        sent(tower_all.at[pl.ds(0, 7 * depth), :], 2)
+        sent(outbox.at[pl.ds(0, groups - 1)], 3)
+        sent(pooled.at[pl.ds(0, 2)], 4)
 
         @pl.when(inner)
         def _():
-            sent(pooled.at[pl.ds(0, 2)], 3)
-
-        sent(biases.at[pl.ds(0, others)], 4)
-
+            sent(pooled.at[pl.ds(0, 2)], 4)
+
+        sent(biases.at[pl.ds(0, others)], 5)
+
+    calls = {
+        "P": pool_out,
+        "A": pool_away,
+        "L": lend,
+        "F": pass_on,
+        "X": narrow,
+    }
+    on_units = {"S": spread, "R": relay, "C": corner}
+    words = {
+        "flip": flip,
+        "widen": widen,
+        "TR": tower_relay,
+        "TC": tower_corner,
+        "SH": share,
+        "E": ready,
+        "Y": lift_first,
+        "end": finish,
+    }
+    do(first_sends)
+    for word in PLAN:
+        if word in words:
+            do(words[word])
+        elif word[0] in on_units:
+            do(on_units[word[0]], *units[int(word[1:])])
+        elif word[0] == "Z":
+            do(lift_last, *map(int, word[1:]))
+        else:
+            do(calls[word[0]], int(word[1:]))
     do(all_sent)
 
 
@@ -481,12 +488,14 @@
             pltpu.VMEM((members, groups, rows, embed), jnp.bfloat16),
             pltpu.VMEM((members, rows * members, block), jnp.bfloat16),
             pltpu.VMEM((members, rows * members, block), jnp.bfloat16),
-            pltpu.VMEM((pieces, width, rank), jnp.bfloat16),
+            pltpu.VMEM((layers, width, rank), jnp.bfloat16),
+            pltpu.VMEM((layers, block, rank), jnp.bfloat16),
+            pltpu.VMEM((layers, members, rank, block), jnp.bfloat16),
             pltpu.VMEM((members, layers, block), jnp.float32),
             pltpu.VMEM((width, units), jnp.bfloat16),
             pltpu.VMEM((1, units), jnp.float32),
             dma((6 + pieces,)),
-            dma((5,)),
+            dma((6,)),
             dma((pieces, members - 1)),
             dma((pieces, members - 1)),
             dma((pieces, members - 1)),

time: 46.9 us -> 34.3 us (0.73)
  Pallas kernels: 45.7 us -> 33.1 us
    pallas_call x1, Pallas kernels: 45.7 us -> 33.1 us  [fused_body(): pl.pallas_call(functools.partial(kernel, groups, members), out_shape=pltp...]
where the time goes in v2:
time: 34.3 us; the launch traced here: 33.9 us
  Pallas kernels  33.1 us (97%)
  local copies, waits for them, and re-layouts  0.71 us (2%)
    pallas_call x1, Pallas kernels, fused_body(): pl.pallas_call(functools.partial(kernel, groups, members), out_shape=pltp...  33.1 us
    unnamed x1, local copies, waits for them, and re-layouts  0.71 us

profile of v2, /device:TPU:0, one launch (start us, length us, event | category | flops | bytes accessed | tf_op | source)
XLA Modules:
  0.0 33.9 jit_solution(1269913940055451537)
XLA Ops:
  0.0 33.1 %shard_map.82 = bf16[256,512]{1,0:T(8,128)(2,1)S(1)} custom-call(s32[8,2048]{1,0:T(8,128)} %bitcast.4, s32[8]{0:T(128)} %order_hbm.1, bf16[1,4096,128]{2,1,0:T(8,128)(2,1)} %table.1, bf16[2,256,512]{2,1,0:T(8,128)(2,1)} %down.1, bf16[2,256,512]{2,1,0:T(8,128)(2,1)} %up.1, f32[2,256]{1,0:T(2,128)} %bias.1, bf16[128,512]{1,0:T(8,128)(2,1)} %tower.1, ...), custom_call_target="tpu_custom_call" | custom-call | tf_op jit(solution)/shard_map/pallas_call | solution.py:476
  33.2 0.7 %copy.10 = bf16[256,512]{1,0:T(8,128)(2,1)} copy(bf16[256,512]{1,0:T(8,128)(2,1)S(1)} %shard_map.82) | data formatting | bytes 524288

commit v3 on v2

--- a/solution.py
+++ b/solution.py
@@ -68,13 +68,14 @@
 VMEM_BYTES = (64 * 1024 - 352) * 1024
 CHIPS = 4
 PLANES = 4
+LANES = 128
 STEPS = (1, 3, 2)
 PLAN = (
-    "flip", "widen", "P1", "P2", "A1", "L1", "P3", "A2", "L3", "P4", "A3", "S0", "S1", "P5",
-    "A4", "P6", "A5", "S2", "P7", "A6", "TR", "P0", "A7", "R0", "R1", "S3", "S4", "R2", "S5",
-    "SH", "R3", "R4", "S6", "R5", "S7", "S8", "C0", "C1", "C2", "TC", "R6", "S9", "R7", "S10",
-    "R8", "S11", "C3", "C4", "C5", "R9", "F1", "R10", "F0", "R11", "C6", "C7", "C8", "E", "X0",
-    "Y", "C9", "C10", "C11", "X1", "Z01", "Z32", "end",
+    "flip", "widen", "P1", "L1", "L3", "P2", "A1", "P3", "A2", "P4", "A3", "P5", "A4", "P6",
+    "A5", "P7", "A6", "P0", "A7", "S0", "S1", "TR", "S2", "S3", "HA", "S4", "S5", "S6", "S7",
+    "R0", "S8", "S9", "R1", "S10", "R2", "S11", "HB", "F1", "R3", "R4", "R5", "F0", "C0", "C1",
+    "C2", "TC", "R6", "R7", "R8", "C3", "C4", "C5", "R9", "R10", "R11", "C6", "C7", "C8", "E",
+    "X0", "Y", "C9", "C10", "C11", "X1", "Z01", "Z32", "end",
 )
 
 
@@ -126,8 +127,8 @@
     chip_z = lax.rem(chip_x + 2, CHIPS)
     chips = (chip_x, chip_y, chip_z)
     layers, block, rank = down.shape
-    hots = ids.shape[0]
     rows, embed = sums.shape
+    hots = ids.shape[0] // (rows * groups * members)
     piece = block // groups
     depth = tower.shape[0]
     pieces = 2 * layers
@@ -157,8 +158,15 @@
     def arrived(ref, recv_sem):
         remote(ref, ref, 0, recv_sem, partner, m).wait_recv()
 
+    half_of = lax.div(m, 2)
+    beside = m + 1 - 2 * lax.rem(m, 2)
+    across = 2 - half_of
+    far_first = 2 * (1 - half_of)
+    inner = jnp.logical_or(m == 1, m == 2)
+    outermost = 3 * (1 - half_of)
+
     def came(k):
-        return wrap(m - k, members)
+        return (m, beside, across, outermost)[k]
 
     def goes(k):
         return wrap(m + k, members)
@@ -200,14 +208,22 @@
     order_copy = load(order_hbm, order, pieces + 4)
     tower_bias_copy = load(tower_bias_hbm, tower_bias, pieces + 5)
 
+    place = 3 - lax.rem(m + half_of, 2)
+
     def lend(p):
-        for k in STEPS:
-            mine = slot(p, m, d)
-            send(mine, mine, p % 2, z_recv.at[p, k - 1], d, goes(k))
+        mine = slot(p, m, d)
+        send(mine, mine, p % 2, z_recv.at[p, place - 1], d, across)
+        send(mine, mine, p % 2, z_recv.at[p, 0], d, beside)
 
     def spread(p, k):
         mine = slot(p, came(k), d)
         arrived(mine, z_recv.at[p, k - 1])
+        if k > 1:
+
+            @pl.when(inner)
+            def _():
+                send(mine, mine, p % 2, z_recv.at[p, k - 1], d, beside)
+
         send(mine, mine, p % 2, plane_recv.at[p, k - 1], chip_x * 2 + c, m)
         send(mine, mine, p % 2, plane_recv.at[p, k - 1], chip_y * 2 + c, m)
         send(mine, mine, p % 2, pair_recv.at[p, k - 1], partner, m)
@@ -252,14 +268,16 @@
     step = 16 if rows % 16 == 0 else 8
 
     def pool(group):
-        first = pl.multiple_of((group * members + m) * rows, rows)
+        first = (group * members + m) * rows
 
         def some(index, carry):
             base = pl.multiple_of(index * step, step)
+            lane = first + base
+            word = lax.div(lane, LANES) * (LANES * hots) + lax.rem(lane, LANES)
             for r in range(step):
                 total = None
                 for hot in range(hots):
-                    at = ids[hot, first + base + r]
+                    at = ids[word + (hot * LANES + r)]
                     row = table_wide[pl.ds(at, 1), :]
                     total = row if total is None else total + row
                 sums[pl.ds(base + r, 1), :] = total
@@ -277,17 +295,12 @@
     def pool_away(i):
         send(outbox.at[i], pooled.at[m, d], 3, pool_recv.at[0], wrap(d + i, groups), m)
 
-    half_of = lax.div(m, 2)
-    beside = m + 1 - 2 * lax.rem(m, 2)
-    across = 2 - half_of
-    far_first = 2 * (1 - half_of)
-    inner = jnp.logical_or(m == 1, m == 2)
-
-    def share():
+    def share_across():
         arrived(outbox.at[pl.ds(0, groups - 1)], pool_recv.at[0])
-        mine = pooled.at[m]
-        send(mine, mine, 4, share_recv.at[m], d, across)
-        send(mine, mine, 4, share_recv.at[m], d, beside)
+        send(pooled.at[m], pooled.at[m], 4, share_recv.at[m], d, across)
+
+    def share_beside():
+        send(pooled.at[m], pooled.at[m], 4, share_recv.at[m], d, beside)
 
     def pass_on(far):
         quarter = m + 2 - 4 * half_of if far else 3 - m
@@ -408,14 +421,17 @@
         remote(ref, ref, which, bias_recv.at[0], partner, m).wait_send()
 
     def all_sent():
-        sent(weights.at[:, pl.ds(0, others * block), :], 0)
-        sent(lifts.at[:, pl.ds(0, others)], 1)
+        total = others * (groups - 1) + 2
+        sent(weights.at[:, pl.ds(0, total * piece), :], 0)
+        sent(weights.at[:, pl.ds(0, total * piece), :], 1)
         sent(tower_all.at[pl.ds(0, 7 * depth), :], 2)
         sent(outbox.at[pl.ds(0, groups - 1)], 3)
         sent(pooled.at[pl.ds(0, 2)], 4)
 
         @pl.when(inner)
         def _():
+            sent(weights.at[:, pl.ds(0, 2 * piece), :], 0)
+            sent(weights.at[:, pl.ds(0, 2 * piece), :], 1)
             sent(pooled.at[pl.ds(0, 2)], 4)
 
         sent(biases.at[pl.ds(0, others)], 5)
@@ -433,7 +449,8 @@
         "widen": widen,
         "TR": tower_relay,
         "TC": tower_corner,
-        "SH": share,
+        "HA": share_across,
+        "HB": share_beside,
         "E": ready,
         "Y": lift_first,
         "end": finish,
@@ -479,7 +496,7 @@
         in_specs=[anywhere] * 8,
         out_specs=vmem,
         scratch_shapes=[
-            pltpu.SMEM((hot_count, batch_size), jnp.int32),
+            pltpu.SMEM((hot_count * batch_size,), jnp.int32),
             pltpu.SMEM(table_of_feature.shape, jnp.int32),
             pltpu.VMEM((vocab, embed), jnp.bfloat16),
             pltpu.VMEM((vocab, embed), jnp.float32),
@@ -509,7 +526,7 @@
             collective_id=0, has_side_effects=True, vmem_limit_bytes=VMEM_BYTES
         ),
     )(
-        feature_ids[0].T,
+        feature_ids[0].reshape(-1, LANES, hot_count).transpose(0, 2, 1).reshape(-1),
         table_of_feature,
         tables,
         cross_down,
@@ -534,7 +551,8 @@
     members = lax.axis_size("mp")
     held = 2 * members * (cross_down.size + cross_up.size) + 2 * groups * tower_weight.size
     placed = groups == 2 * CHIPS and members == PLANES
-    fits = held <= KERNEL_BYTES and placed and tables.shape[0] == 1
+    even = feature_ids.shape[1] % LANES == 0
+    fits = held <= KERNEL_BYTES and placed and even and tables.shape[0] == 1
     chosen = fused_body if fits else plain_body
     return chosen(
         feature_ids,

time: 34.3 us -> 32.3 us (0.942)
  Pallas kernels: 33.1 us -> 31.5 us
    pallas_call x1, Pallas kernels: 33.1 us -> 31.5 us  [fused_body(): pl.pallas_call(functools.partial(kernel, groups, members), out_shape=pltp...]
where the time goes in v3:
time: 32.3 us; the launch traced here: 32.2 us
  Pallas kernels  31.5 us (98%)
  local copies, waits for them, and re-layouts  0.71 us (2%)
    pallas_call x1, Pallas kernels, fused_body(): pl.pallas_call(functools.partial(kernel, groups, members), out_shape=pltp...  31.5 us
    unnamed x1, local copies, waits for them, and re-layouts  0.71 us

profile of v3, /device:TPU:0, one launch (start us, length us, event | category | flops | bytes accessed | tf_op | source)
XLA Modules:
  0.0 32.2 jit_solution(16241478438295797970)
XLA Ops:
  0.0 31.5 %shard_map.82 = bf16[256,512]{1,0:T(8,128)(2,1)S(1)} custom-call(s32[16384]{0:T(1024)} %bitcast.6, s32[8]{0:T(128)} %order_hbm.1, bf16[1,4096,128]{2,1,0:T(8,128)(2,1)} %table.1, bf16[2,256,512]{2,1,0:T(8,128)(2,1)} %down.1, bf16[2,256,512]{2,1,0:T(8,128)(2,1)} %up.1, f32[2,256]{1,0:T(2,128)} %bias.1, bf16[128,512]{1,0:T(8,128)(2,1)} %tower.1, f32[1,512]{1,0:T(1,128)} %bitcast.7), custom_call_target="tpu_custom_call" | custom-call | tf_op jit(solution)/shard_map/pallas_call | solution.py:493
  31.5 0.7 %copy.10 = bf16[256,512]{1,0:T(8,128)(2,1)} copy(bf16[256,512]{1,0:T(8,128)(2,1)S(1)} %shard_map.82) | data formatting | bytes 524288

commit v4 on v3

--- a/solution.py
+++ b/solution.py
@@ -70,12 +70,22 @@
 PLANES = 4
 LANES = 128
 STEPS = (1, 3, 2)
-PLAN = (
-    "flip", "widen", "P1", "L1", "L3", "P2", "A1", "P3", "A2", "P4", "A3", "P5", "A4", "P6",
-    "A5", "P7", "A6", "P0", "A7", "S0", "S1", "TR", "S2", "S3", "HA", "S4", "S5", "S6", "S7",
-    "R0", "S8", "S9", "R1", "S10", "R2", "S11", "HB", "F1", "R3", "R4", "R5", "F0", "C0", "C1",
-    "C2", "TC", "R6", "R7", "R8", "C3", "C4", "C5", "R9", "R10", "R11", "C6", "C7", "C8", "E",
-    "X0", "Y", "C9", "C10", "C11", "X1", "Z01", "Z32", "end",
+FIRST = (
+    "flip", "widen", "P1", "L1", "L2", "L3", "P2", "A1", "P3", "A2", "P4", "A3", "P5", "A4",
+    "P6", "A5", "P7", "A6", "P0", "A7",
+)
+INNER = (
+    "S0", "T1", "T2", "S3", "T4", "T5", "R0", "S6", "T7", "T8", "HA", "S9", "T10", "T11", "HB",
+    "R1", "R2", "R3", "R4", "R5", "F1", "R6", "R7", "R8", "R9", "F0", "R10", "R11", "WR", "C0",
+    "C1", "C2", "C3", "C4", "C5",
+)
+OUTER = (
+    "S0", "S3", "S6", "S9", "HA", "HB", "S1", "S2", "R0", "S4", "S5", "R3", "S7", "S8", "R6",
+    "S10", "S11", "R9", "R1", "R2", "R4", "R5", "R7", "R8", "R10", "R11", "C0", "C3", "WR",
+    "C1", "C2", "C4", "C5",
+)
+LAST = (
+    "C6", "C7", "C8", "E", "X0", "C9", "C10", "C11", "WC", "Y", "X1", "Z", "end",
 )
 
 
@@ -218,12 +228,14 @@
     def spread(p, k):
         mine = slot(p, came(k), d)
         arrived(mine, z_recv.at[p, k - 1])
-        if k > 1:
-
-            @pl.when(inner)
-            def _():
-                send(mine, mine, p % 2, z_recv.at[p, k - 1], d, beside)
-
+        send(mine, mine, p % 2, plane_recv.at[p, k - 1], chip_x * 2 + c, m)
+        send(mine, mine, p % 2, plane_recv.at[p, k - 1], chip_y * 2 + c, m)
+        send(mine, mine, p % 2, pair_recv.at[p, k - 1], partner, m)
+
+    def pass_and_spread(p, k):
+        mine = slot(p, came(k), d)
+        arrived(mine, z_recv.at[p, k - 1])
+        send(mine, mine, p % 2, z_recv.at[p, k - 1], d, beside)
         send(mine, mine, p % 2, plane_recv.at[p, k - 1], chip_x * 2 + c, m)
         send(mine, mine, p % 2, plane_recv.at[p, k - 1], chip_y * 2 + c, m)
         send(mine, mine, p % 2, pair_recv.at[p, k - 1], partner, m)
@@ -304,12 +316,9 @@
 
     def pass_on(far):
         quarter = m + 2 - 4 * half_of if far else 3 - m
-
-        @pl.when(inner)
-        def _():
-            theirs = pooled.at[quarter]
-            arrived(theirs, share_recv.at[quarter])
-            send(theirs, theirs, 4, share_recv.at[quarter], d, beside)
+        theirs = pooled.at[quarter]
+        arrived(theirs, share_recv.at[quarter])
+        send(theirs, theirs, 4, share_recv.at[quarter], d, beside)
 
     def shared():
         arrived(pooled.at[beside], share_recv.at[beside])
@@ -349,8 +358,7 @@
         value = wide * (lifted + biases[b, layer : layer + 1, :]) + state[b].astype(jnp.float32)
         return value.astype(jnp.bfloat16)
 
-    order_of = tuple(range(0, pieces - 1, 2)) + tuple(range(1, pieces, 2))
-    units = [(p, k) for p in order_of for k in STEPS]
+    units = [(p, k) for p in range(pieces) for k in STEPS]
 
     def do(call, *args):
         with jax.named_scope(call.__name__ + "_".join(map(str, args))):
@@ -358,15 +366,15 @@
 
     def first_sends():
         tower_copy.wait()
-        for copy in weight_copies:
-            copy.wait()
-        bias_copy.wait()
         pl.semaphore_wait(barrier, members - 1 + groups - 1)
         tower_spread()
+        weight_copies[0].wait()
         lend(0)
+        bias_copy.wait()
         for k in range(1, members):
             send(biases.at[m], biases.at[m], 5, bias_recv.at[0], d, goes(k))
-        lend(2)
+        for copy in weight_copies[1:]:
+            copy.wait()
 
     def flip():
         for n in range(layers):
@@ -396,26 +404,24 @@
         for b in range(members):
             crossed[b] = lift(0, state["projected"], b)
 
-    def lift_last(*steps):
-        for k in steps:
-            if k:
-                complete(pieces - 1, k)
-            else:
-                tower_bias_copy.wait()
-                arrived(tower_all.at[pl.ds(0, CHIPS * depth), :], tower_recv.at[2])
-        for k in steps:
-            b = came(k)
-            value = lift(layers - 1, state["projected"], b)
+    def lift_last():
+        for k in STEPS:
+            complete(pieces - 1, k)
+        for b in range(members):
+            crossed[b] = lift(layers - 1, state["projected"], b)
+
+    def finish():
+        tower_bias_copy.wait()
+        arrived(tower_all.at[pl.ds(0, CHIPS * depth), :], tower_recv.at[2])
+        total = None
+        for b in range(members):
             part = jnp.dot(
-                value,
-                tower_all[pl.ds(pl.multiple_of(b * block, block), block), :],
+                crossed[b],
+                tower_all[b * block : (b + 1) * block, :],
                 preferred_element_type=jnp.float32,
             )
-            state["answer"] = state["answer"] + part if "answer" in state else part
-
-    def finish():
-        total = state["answer"] + tower_bias[...]
-        out[...] = jnp.maximum(total, 0.0).astype(jnp.bfloat16)
+            total = part if total is None else total + part
+        out[...] = jnp.maximum(total + tower_bias[...], 0.0).astype(jnp.bfloat16)
 
     def sent(ref, which):
         remote(ref, ref, which, bias_recv.at[0], partner, m).wait_send()
@@ -443,28 +449,40 @@
         "F": pass_on,
         "X": narrow,
     }
-    on_units = {"S": spread, "R": relay, "C": corner}
+    on_units = {"S": spread, "T": pass_and_spread, "R": relay, "C": corner}
     words = {
         "flip": flip,
         "widen": widen,
-        "TR": tower_relay,
-        "TC": tower_corner,
+        "WR": tower_relay,
+        "WC": tower_corner,
         "HA": share_across,
         "HB": share_beside,
         "E": ready,
         "Y": lift_first,
+        "Z": lift_last,
         "end": finish,
     }
+    def follow(plan):
+        for word in plan:
+            if word in words:
+                do(words[word])
+            elif word[0] in on_units:
+                do(on_units[word[0]], *units[int(word[1:])])
+            else:
+                do(calls[word[0]], int(word[1:]))
+
     do(first_sends)
-    for word in PLAN:
-        if word in words:
-            do(words[word])
-        elif word[0] in on_units:
-            do(on_units[word[0]], *units[int(word[1:])])
-        elif word[0] == "Z":
-            do(lift_last, *map(int, word[1:]))
-        else:
-            do(calls[word[0]], int(word[1:]))
+    follow(FIRST)
+
+    @pl.when(inner)
+    def _():
+        follow(INNER)
+
+    @pl.when(jnp.logical_not(inner))
+    def _():
+        follow(OUTER)
+
+    follow(LAST)
     do(all_sent)
 
 

time: 32.3 us -> 29.7 us (0.920)
  Pallas kernels: 31.5 us -> 28.8 us
    pallas_call x1, Pallas kernels: 31.5 us -> 28.8 us  [fused_body(): pl.pallas_call(functools.partial(kernel, groups, members), out_shape=pltp...]
where the time goes in v4:
time: 29.7 us; the launch traced here: 29.5 us
  Pallas kernels  28.8 us (97%)
  local copies, waits for them, and re-layouts  0.71 us (2%)
    pallas_call x1, Pallas kernels, fused_body(): pl.pallas_call(functools.partial(kernel, groups, members), out_shape=pltp...  28.8 us
    unnamed x1, local copies, waits for them, and re-layouts  0.71 us

profile of v4, /device:TPU:0, one launch (start us, length us, event | category | flops | bytes accessed | tf_op | source)
XLA Modules:
  0.0 29.5 jit_solution(6805256817069353455)
XLA Ops:
  0.0 28.8 %shard_map.82 = bf16[256,512]{1,0:T(8,128)(2,1)S(1)} custom-call(s32[16384]{0:T(1024)} %bitcast.6, s32[8]{0:T(128)} %order_hbm.1, bf16[1,4096,128]{2,1,0:T(8,128)(2,1)} %table.1, bf16[2,256,512]{2,1,0:T(8,128)(2,1)} %down.1, bf16[2,256,512]{2,1,0:T(8,128)(2,1)} %up.1, f32[2,256]{1,0:T(2,128)} %bias.1, bf16[128,512]{1,0:T(8,128)(2,1)} %tower.1, f32[1,512]{1,0:T(1,128)} %bitcast.7), custom_call_target="tpu_custom_call" | custom-call | tf_op jit(solution)/shard_map/pallas_call | solution.py:511
  28.8 0.7 %copy.10 = bf16[256,512]{1,0:T(8,128)(2,1)} copy(bf16[256,512]{1,0:T(8,128)(2,1)S(1)} %shard_map.82) | data formatting | bytes 524288

commit v5 on v4

--- a/solution.py
+++ b/solution.py
@@ -71,21 +71,21 @@
 LANES = 128
 STEPS = (1, 3, 2)
 FIRST = (
-    "flip", "widen", "P1", "L1", "L2", "L3", "P2", "A1", "P3", "A2", "P4", "A3", "P5", "A4",
-    "P6", "A5", "P7", "A6", "P0", "A7",
+    "flip", "widen", "P6", "L1", "L2", "L3", "P7", "A6", "P4", "A7", "P5", "A4", "P2", "A5",
+    "P3", "A2", "P1", "A3", "P0", "A1",
 )
 INNER = (
-    "S0", "T1", "T2", "S3", "T4", "T5", "R0", "S6", "T7", "T8", "HA", "S9", "T10", "T11", "HB",
-    "R1", "R2", "R3", "R4", "R5", "F1", "R6", "R7", "R8", "R9", "F0", "R10", "R11", "WR", "C0",
-    "C1", "C2", "C3", "C4", "C5",
+    "S0", "T1", "T2", "S3", "T4", "T5", "G1", "R0", "S6", "T7", "T8", "G0", "S9", "T10", "T11",
+    "H1", "H0", "R1", "R2", "R3", "F11", "R4", "R5", "F10", "F01", "R6", "R7", "R8", "R9",
+    "F00", "R10", "R11", "WR", "C0", "C1", "C2", "C3", "C4", "C5",
 )
 OUTER = (
-    "S0", "S3", "S6", "S9", "HA", "HB", "S1", "S2", "R0", "S4", "S5", "R3", "S7", "S8", "R6",
-    "S10", "S11", "R9", "R1", "R2", "R4", "R5", "R7", "R8", "R10", "R11", "C0", "C3", "WR",
-    "C1", "C2", "C4", "C5",
+    "S0", "S3", "S6", "S9", "G1", "H1", "G0", "H0", "S1", "S2", "R0", "S4", "S5", "R3", "S7",
+    "S8", "R6", "S10", "S11", "R9", "R1", "R2", "R4", "R5", "R7", "R8", "R10", "R11", "WR",
+    "C0", "C3", "C1", "C2", "C4", "C5",
 )
 LAST = (
-    "C6", "C7", "C8", "E", "X0", "C9", "C10", "C11", "WC", "Y", "X1", "Z", "end",
+    "C6", "C7", "C8", "C9", "C10", "C11", "E", "X0", "WC", "Y", "X1", "Z", "near", "end",
 )
 
 
@@ -275,7 +275,7 @@
     def tower_corner():
         far = tower_slot(chip_z * 2 + c)
         arrived(far, tower_recv.at[1])
-        send(far, far, 2, tower_recv.at[2], partner, m)
+        send(far, far, 2, tower_recv.at[3], partner, m)
 
     step = 16 if rows % 16 == 0 else 8
 
@@ -298,42 +298,52 @@
         lax.fori_loop(0, rows // step, some, 0)
         return sums[...].astype(jnp.bfloat16)
 
-    def pool_out(i):
-        if i == 0:
-            pooled[m, d] = pool(d)
+    def related(j):
+        return (q, chip_x, chip_y, chip_z)[j // 2] * 2 + (c if j % 2 == 0 else 1 - c)
+
+    def pool_out(j):
+        if j == 0:
+            pooled[m, 0] = pool(d)
         else:
-            outbox[i] = pool(wrap(d + i, groups))
-
-    def pool_away(i):
-        send(outbox.at[i], pooled.at[m, d], 3, pool_recv.at[0], wrap(d + i, groups), m)
-
-    def share_across():
-        arrived(outbox.at[pl.ds(0, groups - 1)], pool_recv.at[0])
-        send(pooled.at[m], pooled.at[m], 4, share_recv.at[m], d, across)
-
-    def share_beside():
-        send(pooled.at[m], pooled.at[m], 4, share_recv.at[m], d, beside)
-
-    def pass_on(far):
+            outbox[j] = pool(related(j))
+
+    def pool_away(j):
+        send(outbox.at[j], pooled.at[m, j], 3, pool_recv.at[j // CHIPS], related(j), m)
+
+    def part(quarter, half):
+        return pooled.at[quarter, pl.ds(half * CHIPS, CHIPS)]
+
+    def share_across(half):
+        arrived(outbox.at[pl.ds(0, CHIPS - 1 + half)], pool_recv.at[half])
+        mine = part(m, half)
+        send(mine, mine, 4, share_recv.at[m, half], d, across)
+
+    def share_beside(half):
+        mine = part(m, half)
+        send(mine, mine, 4, share_recv.at[m, half], d, beside)
+
+    def pass_on(far, half):
         quarter = m + 2 - 4 * half_of if far else 3 - m
-        theirs = pooled.at[quarter]
-        arrived(theirs, share_recv.at[quarter])
-        send(theirs, theirs, 4, share_recv.at[quarter], d, beside)
+        theirs = part(quarter, half)
+        arrived(theirs, share_recv.at[quarter, half])
+        send(theirs, theirs, 4, share_recv.at[quarter, half], d, beside)
 
     def shared():
-        arrived(pooled.at[beside], share_recv.at[beside])
+        for half in range(2):
+            arrived(part(beside, half), share_recv.at[beside, half])
 
         @pl.when(jnp.logical_not(inner))
         def _():
             for j in range(2):
-                arrived(pooled.at[far_first + j], share_recv.at[far_first + j])
+                for half in range(2):
+                    arrived(part(far_first + j, half), share_recv.at[far_first + j, half])
 
     def embed_all():
         per_block = block // embed
         order_copy.wait()
         for b in range(members):
             for f in range(per_block):
-                at = order[b * per_block + f]
+                at = lax.bitwise_xor(order[b * per_block + f], d)
                 for quarter in range(members):
                     embedded[
                         b, quarter * rows : (quarter + 1) * rows, f * embed : (f + 1) * embed
@@ -410,17 +420,18 @@
         for b in range(members):
             crossed[b] = lift(layers - 1, state["projected"], b)
 
+    def tower_term(b):
+        rows_of = pl.ds(pl.multiple_of(b * block, block), block)
+        return jnp.dot(crossed[b], tower_all[rows_of, :], preferred_element_type=jnp.float32)
+
+    def near_terms():
+        tower_bias_copy.wait()
+        arrived(tower_all.at[pl.ds(0, (CHIPS - 1) * depth), :], tower_recv.at[2])
+        state["total"] = tower_term(q) + tower_term(chip_x) + tower_term(chip_y)
+
     def finish():
-        tower_bias_copy.wait()
-        arrived(tower_all.at[pl.ds(0, CHIPS * depth), :], tower_recv.at[2])
-        total = None
-        for b in range(members):
-            part = jnp.dot(
-                crossed[b],
-                tower_all[b * block : (b + 1) * block, :],
-                preferred_element_type=jnp.float32,
-            )
-            total = part if total is None else total + part
+        arrived(tower_slot(chip_z * 2 + 1 - c), tower_recv.at[3])
+        total = state["total"] + tower_term(chip_z)
         out[...] = jnp.maximum(total + tower_bias[...], 0.0).astype(jnp.bfloat16)
 
     def sent(ref, which):
@@ -447,6 +458,8 @@
         "A": pool_away,
         "L": lend,
         "F": pass_on,
+        "G": share_across,
+        "H": share_beside,
         "X": narrow,
     }
     on_units = {"S": spread, "T": pass_and_spread, "R": relay, "C": corner}
@@ -455,11 +468,10 @@
         "widen": widen,
         "WR": tower_relay,
         "WC": tower_corner,
-        "HA": share_across,
-        "HB": share_beside,
         "E": ready,
         "Y": lift_first,
         "Z": lift_last,
+        "near": near_terms,
         "end": finish,
     }
     def follow(plan):
@@ -469,7 +481,7 @@
             elif word[0] in on_units:
                 do(on_units[word[0]], *units[int(word[1:])])
             else:
-                do(calls[word[0]], int(word[1:]))
+                do(calls[word[0]], *map(int, word[1:]))
 
     do(first_sends)
     follow(FIRST)
@@ -535,9 +547,9 @@
             dma((pieces, members - 1)),
             dma((pieces, members - 1)),
             dma((pieces, members - 1)),
-            dma((3,)),
-            dma((1,)),
-            dma((members,)),
+            dma((4,)),
+            dma((2,)),
+            dma((members, 2)),
             dma((1,)),
         ],
         compiler_params=pltpu.CompilerParams(

time: 29.7 us -> 29.3 us (0.987)
  Pallas kernels: 28.8 us -> 28.4 us
    pallas_call x1, Pallas kernels: 28.8 us -> 28.4 us  [fused_body(): pl.pallas_call(functools.partial(kernel, groups, members), out_shape=pltp...]
where the time goes in v5:
time: 29.3 us; the launch traced here: 29.1 us
  Pallas kernels  28.4 us (97%)
  local copies, waits for them, and re-layouts  0.71 us (2%)
    pallas_call x1, Pallas kernels, fused_body(): pl.pallas_call(functools.partial(kernel, groups, members), out_shape=pltp...  28.4 us
    unnamed x1, local copies, waits for them, and re-layouts  0.71 us

profile of v5, /device:TPU:0, one launch (start us, length us, event | category | flops | bytes accessed | tf_op | source)
XLA Modules:
  0.0 29.1 jit_solution(12186606862960488035)
XLA Ops:
  0.0 28.4 %shard_map.82 = bf16[256,512]{1,0:T(8,128)(2,1)S(1)} custom-call(s32[16384]{0:T(1024)} %bitcast.6, s32[8]{0:T(128)} %order_hbm.1, bf16[1,4096,128]{2,1,0:T(8,128)(2,1)} %table.1, bf16[2,256,512]{2,1,0:T(8,128)(2,1)} %down.1, bf16[2,256,512]{2,1,0:T(8,128)(2,1)} %up.1, f32[2,256]{1,0:T(2,128)} %bias.1, bf16[128,512]{1,0:T(8,128)(2,1)} %tower.1, f32[1,512]{1,0:T(1,128)} %bitcast.7), custom_call_target="tpu_custom_call" | custom-call | tf_op jit(solution)/shard_map/pallas_call | solution.py:523
  28.4 0.7 %copy.10 = bf16[256,512]{1,0:T(8,128)(2,1)} copy(bf16[256,512]{1,0:T(8,128)(2,1)S(1)} %shard_map.82) | data formatting | bytes 524288

commit v6 on v5

--- a/solution.py
+++ b/solution.py
@@ -72,20 +72,19 @@
 STEPS = (1, 3, 2)
 FIRST = (
     "flip", "widen", "P6", "L1", "L2", "L3", "P7", "A6", "P4", "A7", "P5", "A4", "P2", "A5",
-    "P3", "A2", "P1", "A3", "P0", "A1",
 )
 INNER = (
-    "S0", "T1", "T2", "S3", "T4", "T5", "G1", "R0", "S6", "T7", "T8", "G0", "S9", "T10", "T11",
-    "H1", "H0", "R1", "R2", "R3", "F11", "R4", "R5", "F10", "F01", "R6", "R7", "R8", "R9",
-    "F00", "R10", "R11", "WR", "C0", "C1", "C2", "C3", "C4", "C5",
+    "P3", "A2", "P1", "A3", "T1", "T2", "P0", "A1", "S0", "T4", "T5", "S3", "G1", "T7", "T8",
+    "G0", "S6", "T10", "T11", "S9", "H1", "H0", "R0", "R1", "R2", "R3", "F11", "R4", "R5",
+    "F10", "F01", "R6", "R7", "R8", "R9", "F00", "R10", "R11", "WR", "C0", "C1",
 )
 OUTER = (
-    "S0", "S3", "S6", "S9", "G1", "H1", "G0", "H0", "S1", "S2", "R0", "S4", "S5", "R3", "S7",
-    "S8", "R6", "S10", "S11", "R9", "R1", "R2", "R4", "R5", "R7", "R8", "R10", "R11", "WR",
-    "C0", "C3", "C1", "C2", "C4", "C5",
+    "P3", "A2", "S0", "P1", "A3", "S3", "P0", "A1", "S6", "S9", "G1", "H1", "G0", "H0", "S1",
+    "S2", "R0", "S4", "S5", "R3", "S7", "S8", "R6", "S10", "S11", "R9", "R1", "R2", "R4", "R5",
+    "R7", "R8", "R10", "R11", "WR", "C0", "C1",
 )
 LAST = (
-    "C6", "C7", "C8", "C9", "C10", "C11", "E", "X0", "WC", "Y", "X1", "Z", "near", "end",
+    "C2", "C3", "E", "X0", "Y", "WC", "X1", "Z", "near", "end",
 )
 
 
@@ -192,10 +191,8 @@
             return weights.at[p // 2, pl.ds(pl.multiple_of(start, length), length), :]
         return lifts.at[p // 2, member, pl.ds(pl.multiple_of(start, length), length), :]
 
-    def amount(p, count):
-        if p % 2 == 0:
-            return weights.at[p // 2, pl.ds(0, count * piece), :]
-        return lifts.at[p // 2, 0, pl.ds(0, count * thin), :]
+    def amount(count):
+        return weights.at[0, pl.ds(0, count * piece), :]
 
     def tower_slot(device, half=None):
         length = depth if half is None else depth // 2
@@ -210,13 +207,13 @@
 
     here = pl.ds(pl.multiple_of(m * block, block), block)
     tower_copy = load(tower, tower_slot(d), 0)
-    weight_copies = [load(down.at[n], weights.at[n, here, :], 1 + n) for n in range(layers)]
-    up_copies = [load(up.at[n], up_raw.at[n], 1 + layers + n) for n in range(layers)]
-    table_copy = load(table.at[0], table_half, pieces + 1)
-    ids_copy = load(ids_hbm, ids, pieces + 2)
-    bias_copy = load(bias, biases.at[m], pieces + 3)
-    order_copy = load(order_hbm, order, pieces + 4)
-    tower_bias_copy = load(tower_bias_hbm, tower_bias, pieces + 5)
+    down_copy = load(down, weights.at[:, here, :], 1)
+    up_copy = load(up, up_raw, 2)
+    table_copy = load(table.at[0], table_half, 3)
+    ids_copy = load(ids_hbm, ids, 4)
+    bias_copy = load(bias, biases.at[m], 5)
+    order_copy = load(order_hbm, order, 6)
+    tower_bias_copy = load(tower_bias_hbm, tower_bias, 7)
 
     place = 3 - lax.rem(m + half_of, 2)
 
@@ -230,7 +227,7 @@
         arrived(mine, z_recv.at[p, k - 1])
         send(mine, mine, p % 2, plane_recv.at[p, k - 1], chip_x * 2 + c, m)
         send(mine, mine, p % 2, plane_recv.at[p, k - 1], chip_y * 2 + c, m)
-        send(mine, mine, p % 2, pair_recv.at[p, k - 1], partner, m)
+        send(mine, mine, p % 2, pair_recv.at[p], partner, m)
 
     def pass_and_spread(p, k):
         mine = slot(p, came(k), d)
@@ -238,24 +235,25 @@
         send(mine, mine, p % 2, z_recv.at[p, k - 1], d, beside)
         send(mine, mine, p % 2, plane_recv.at[p, k - 1], chip_x * 2 + c, m)
         send(mine, mine, p % 2, plane_recv.at[p, k - 1], chip_y * 2 + c, m)
-        send(mine, mine, p % 2, pair_recv.at[p, k - 1], partner, m)
+        send(mine, mine, p % 2, pair_recv.at[p], partner, m)
 
     def relay(p, k):
-        arrived(amount(p, 2), plane_recv.at[p, k - 1])
+        arrived(amount(2), plane_recv.at[p, k - 1])
         for j in range(2):
             half = slot(p, came(k), chips[j] * 2 + c, j)
-            send(half, half, p % 2, diag_recv.at[p, k - 1], chips[1 - j] * 2 + c, m)
+            send(half, half, p % 2, diag_recv.at[p], chips[1 - j] * 2 + c, m)
         for j in range(2):
             whole = slot(p, came(k), chips[j] * 2 + c)
-            send(whole, whole, p % 2, pair_recv.at[p, k - 1], partner, m)
-
-    def corner(p, k):
-        far = slot(p, came(k), chip_z * 2 + c)
-        arrived(far, diag_recv.at[p, k - 1])
-        send(far, far, p % 2, pair_recv.at[p, k - 1], partner, m)
-
-    def complete(p, k):
-        arrived(amount(p, CHIPS), pair_recv.at[p, k - 1])
+            send(whole, whole, p % 2, pair_recv.at[p], partner, m)
+
+    def corner(p):
+        arrived(amount(others), diag_recv.at[p])
+        for k in STEPS:
+            far = slot(p, came(k), chip_z * 2 + c)
+            send(far, far, p % 2, pair_recv.at[p], partner, m)
+
+    def complete(p):
+        arrived(amount(CHIPS * others), pair_recv.at[p])
 
     def tower_spread():
         mine = tower_slot(d)
@@ -378,17 +376,15 @@
         tower_copy.wait()
         pl.semaphore_wait(barrier, members - 1 + groups - 1)
         tower_spread()
-        weight_copies[0].wait()
+        down_copy.wait()
         lend(0)
         bias_copy.wait()
         for k in range(1, members):
             send(biases.at[m], biases.at[m], 5, bias_recv.at[0], d, goes(k))
-        for copy in weight_copies[1:]:
-            copy.wait()
 
     def flip():
+        up_copy.wait()
         for n in range(layers):
-            up_copies[n].wait()
             lifts[n, m] = up_raw[n].T
 
     def widen():
@@ -404,19 +400,16 @@
         arrived(biases.at[pl.ds(0, others)], bias_recv.at[0])
 
     def narrow(layer):
-        for k in STEPS:
-            complete(2 * layer, k)
+        complete(2 * layer)
         state["projected"] = project(layer)
 
     def lift_first():
-        for k in STEPS:
-            complete(1, k)
+        complete(1)
         for b in range(members):
             crossed[b] = lift(0, state["projected"], b)
 
     def lift_last():
-        for k in STEPS:
-            complete(pieces - 1, k)
+        complete(pieces - 1)
         for b in range(members):
             crossed[b] = lift(layers - 1, state["projected"], b)
 
@@ -457,12 +450,13 @@
         "P": pool_out,
         "A": pool_away,
         "L": lend,
+        "C": corner,
         "F": pass_on,
         "G": share_across,
         "H": share_beside,
         "X": narrow,
     }
-    on_units = {"S": spread, "T": pass_and_spread, "R": relay, "C": corner}
+    on_units = {"S": spread, "T": pass_and_spread, "R": relay}
     words = {
         "flip": flip,
         "widen": widen,
@@ -541,12 +535,12 @@
             pltpu.VMEM((members, layers, block), jnp.float32),
             pltpu.VMEM((width, units), jnp.bfloat16),
             pltpu.VMEM((1, units), jnp.float32),
-            dma((6 + pieces,)),
+            dma((8,)),
             dma((6,)),
             dma((pieces, members - 1)),
             dma((pieces, members - 1)),
-            dma((pieces, members - 1)),
-            dma((pieces, members - 1)),
+            dma((pieces,)),
+            dma((pieces,)),
             dma((4,)),
             dma((2,)),
             dma((members, 2)),

time: 29.3 us -> 28.9 us (0.986)
  Pallas kernels: 28.4 us -> 28 us
    pallas_call x1, Pallas kernels: 28.4 us -> 28 us  [fused_body(): pl.pallas_call(functools.partial(kernel, groups, members), out_shape=pltp...]
where the time goes in v6:
time: 28.9 us; the launch traced here: 28.7 us
  Pallas kernels  28 us (97%)
  local copies, waits for them, and re-layouts  0.71 us (2%)
    pallas_call x1, Pallas kernels, fused_body(): pl.pallas_call(functools.partial(kernel, groups, members), out_shape=pltp...  28 us
    unnamed x1, local copies, waits for them, and re-layouts  0.71 us

profile of v6, /device:TPU:0, one launch (start us, length us, event | category | flops | bytes accessed | tf_op | source)
XLA Modules:
  0.0 28.7 jit_solution(14457094624550450978)
XLA Ops:
  0.0 28.0 %shard_map.82 = bf16[256,512]{1,0:T(8,128)(2,1)S(1)} custom-call(s32[16384]{0:T(1024)} %bitcast.6, s32[8]{0:T(128)} %order_hbm.1, bf16[1,4096,128]{2,1,0:T(8,128)(2,1)} %table.1, bf16[2,256,512]{2,1,0:T(8,128)(2,1)} %down.1, bf16[2,256,512]{2,1,0:T(8,128)(2,1)} %up.1, f32[2,256]{1,0:T(2,128)} %bias.1, bf16[128,512]{1,0:T(8,128)(2,1)} %tower.1, f32[1,512]{1,0:T(1,128)} %bitcast.7), custom_call_target="tpu_custom_call" | custom-call | tf_op jit(solution)/shard_map/pallas_call | solution.py:517
  28.0 0.7 %copy.10 = bf16[256,512]{1,0:T(8,128)(2,1)} copy(bf16[256,512]{1,0:T(8,128)(2,1)S(1)} %shard_map.82) | data formatting | bytes 524288

commit v7 on v6

--- a/solution.py
+++ b/solution.py
@@ -75,16 +75,16 @@
 )
 INNER = (
     "P3", "A2", "P1", "A3", "T1", "T2", "P0", "A1", "S0", "T4", "T5", "S3", "G1", "T7", "T8",
-    "G0", "S6", "T10", "T11", "S9", "H1", "H0", "R0", "R1", "R2", "R3", "F11", "R4", "R5",
+    "G0", "S6", "T10", "T11", "S9", "H1", "H0", "WP", "R0", "R1", "R2", "R3", "F11", "R4", "R5",
     "F10", "F01", "R6", "R7", "R8", "R9", "F00", "R10", "R11", "WR", "C0", "C1",
 )
 OUTER = (
-    "P3", "A2", "S0", "P1", "A3", "S3", "P0", "A1", "S6", "S9", "G1", "H1", "G0", "H0", "S1",
-    "S2", "R0", "S4", "S5", "R3", "S7", "S8", "R6", "S10", "S11", "R9", "R1", "R2", "R4", "R5",
-    "R7", "R8", "R10", "R11", "WR", "C0", "C1",
+    "P3", "A2", "S0", "P1", "A3", "S3", "P0", "A1", "S6", "S9", "G1", "H1", "G0", "H0", "WP",
+    "S1", "S2", "R0", "S4", "S5", "R3", "S7", "S8", "R6", "S10", "S11", "R9", "R1", "R2", "R4",
+    "R5", "R7", "R8", "R10", "R11", "WR", "C0", "C1",
 )
 LAST = (
-    "C2", "C3", "E", "X0", "Y", "WC", "X1", "Z", "near", "end",
+    "C2", "C3", "E", "X0", "Y", "WC", "X1", "Z", "end",
 )
 
 
@@ -199,15 +199,15 @@
         start = device * depth + (0 if half is None else half * length)
         return tower_all.at[pl.ds(pl.multiple_of(start, length), length), :]
 
+    here = pl.ds(pl.multiple_of(m * block, block), block)
+    tower_copy = load(tower, tower_slot(d), 0)
+    down_copy = load(down, weights.at[:, here, :], 1)
     barrier = pltpu.get_barrier_semaphore()
     for k in range(1, members):
         pl.semaphore_signal(barrier, inc=1, device_id=(d, goes(k)), device_id_type=MESH)
     for i in range(1, groups):
         pl.semaphore_signal(barrier, inc=1, device_id=(wrap(d + i, groups), m), device_id_type=MESH)
 
-    here = pl.ds(pl.multiple_of(m * block, block), block)
-    tower_copy = load(tower, tower_slot(d), 0)
-    down_copy = load(down, weights.at[:, here, :], 1)
     up_copy = load(up, up_raw, 2)
     table_copy = load(table.at[0], table_half, 3)
     ids_copy = load(ids_hbm, ids, 4)
@@ -261,19 +261,27 @@
         send(mine, mine, 2, tower_recv.at[0], chip_y * 2 + c, m)
         send(mine, mine, 2, tower_recv.at[2], partner, m)
 
-    def tower_relay():
+    def tower_pair():
         arrived(tower_all.at[pl.ds(0, 2 * depth), :], tower_recv.at[0])
-        for j in range(2):
-            half = tower_slot(chips[j] * 2 + c, j)
-            send(half, half, 2, tower_recv.at[1], chips[1 - j] * 2 + c, m)
         for j in range(2):
             whole = tower_slot(chips[j] * 2 + c)
             send(whole, whole, 2, tower_recv.at[2], partner, m)
 
+    def tower_relay():
+        @pl.when(c == 1)
+        def _():
+            arrived(tower_all.at[pl.ds(0, 3 * depth), :], tower_recv.at[2])
+            for core in range(2):
+                for j in range(2):
+                    half = tower_slot(chips[j] * 2 + core, j)
+                    send(half, half, 2, tower_recv.at[1], chips[1 - j] * 2 + c, m)
+
     def tower_corner():
-        far = tower_slot(chip_z * 2 + c)
-        arrived(far, tower_recv.at[1])
-        send(far, far, 2, tower_recv.at[3], partner, m)
+        @pl.when(c == 1)
+        def _():
+            far = tower_all.at[pl.ds(pl.multiple_of(chip_z * block, block), block), :]
+            arrived(far, tower_recv.at[1])
+            send(far, far, 2, tower_recv.at[3], partner, m)
 
     step = 16 if rows % 16 == 0 else 8
 
@@ -326,45 +334,36 @@
         arrived(theirs, share_recv.at[quarter, half])
         send(theirs, theirs, 4, share_recv.at[quarter, half], d, beside)
 
-    def shared():
+    def ready_all():
         for half in range(2):
             arrived(part(beside, half), share_recv.at[beside, half])
 
         @pl.when(jnp.logical_not(inner))
         def _():
-            for j in range(2):
+            for quarter in (outermost, across):
                 for half in range(2):
-                    arrived(part(far_first + j, half), share_recv.at[far_first + j, half])
-
-    def embed_all():
-        per_block = block // embed
+                    arrived(part(quarter, half), share_recv.at[quarter, half])
+
         order_copy.wait()
-        for b in range(members):
-            for f in range(per_block):
-                at = lax.bitwise_xor(order[b * per_block + f], d)
-                for quarter in range(members):
-                    embedded[
-                        b, quarter * rows : (quarter + 1) * rows, f * embed : (f + 1) * embed
-                    ] = pooled[quarter, at]
+        arrived(biases.at[pl.ds(0, others)], bias_recv.at[0])
+        for f in range(groups):
+            at = lax.bitwise_xor(order[f], d)
+            for quarter in range(members):
+                here = slice(quarter * rows, (quarter + 1) * rows)
+                embedded[here, f * embed : (f + 1) * embed] = pooled[quarter, at]
 
     def project(layer):
         state = embedded if layer == 0 else crossed
-        value = None
-        for b in range(members):
-            term = jnp.dot(
-                state[b],
-                weights[layer, b * block : (b + 1) * block, :],
-                preferred_element_type=jnp.float32,
-            )
-            value = term if value is None else value + term
+        value = jnp.dot(state[...], weights[layer], preferred_element_type=jnp.float32)
         return value.astype(jnp.bfloat16)
 
     def lift(layer, projected, b):
         state = embedded if layer == 0 else crossed
+        here = slice(b * block, (b + 1) * block)
         lifted = jnp.dot(projected, lifts[layer, b], preferred_element_type=jnp.float32)
-        wide = embedded[b].astype(jnp.float32)
-        value = wide * (lifted + biases[b, layer : layer + 1, :]) + state[b].astype(jnp.float32)
-        return value.astype(jnp.bfloat16)
+        wide = embedded[:, here].astype(jnp.float32)
+        value = wide * (lifted + biases[b, layer : layer + 1, :])
+        crossed[:, here] = (value + state[:, here].astype(jnp.float32)).astype(jnp.bfloat16)
 
     units = [(p, k) for p in range(pieces) for k in STEPS]
 
@@ -394,11 +393,6 @@
 
     state = {}
 
-    def ready():
-        shared()
-        embed_all()
-        arrived(biases.at[pl.ds(0, others)], bias_recv.at[0])
-
     def narrow(layer):
         complete(2 * layer)
         state["projected"] = project(layer)
@@ -406,25 +400,22 @@
     def lift_first():
         complete(1)
         for b in range(members):
-            crossed[b] = lift(0, state["projected"], b)
+            lift(0, state["projected"], b)
 
     def lift_last():
         complete(pieces - 1)
         for b in range(members):
-            crossed[b] = lift(layers - 1, state["projected"], b)
-
-    def tower_term(b):
-        rows_of = pl.ds(pl.multiple_of(b * block, block), block)
-        return jnp.dot(crossed[b], tower_all[rows_of, :], preferred_element_type=jnp.float32)
-
-    def near_terms():
+            lift(layers - 1, state["projected"], b)
+
+    def finish():
         tower_bias_copy.wait()
-        arrived(tower_all.at[pl.ds(0, (CHIPS - 1) * depth), :], tower_recv.at[2])
-        state["total"] = tower_term(q) + tower_term(chip_x) + tower_term(chip_y)
-
-    def finish():
-        arrived(tower_slot(chip_z * 2 + 1 - c), tower_recv.at[3])
-        total = state["total"] + tower_term(chip_z)
+
+        @pl.when(c == 0)
+        def _():
+            arrived(tower_all.at[pl.ds(0, 3 * depth), :], tower_recv.at[2])
+            arrived(tower_all.at[pl.ds(0, block), :], tower_recv.at[3])
+
+        total = jnp.dot(crossed[...], tower_all[...], preferred_element_type=jnp.float32)
         out[...] = jnp.maximum(total + tower_bias[...], 0.0).astype(jnp.bfloat16)
 
     def sent(ref, which):
@@ -434,7 +425,12 @@
         total = others * (groups - 1) + 2
         sent(weights.at[:, pl.ds(0, total * piece), :], 0)
         sent(weights.at[:, pl.ds(0, total * piece), :], 1)
-        sent(tower_all.at[pl.ds(0, 7 * depth), :], 2)
+        sent(tower_all.at[pl.ds(0, 5 * depth), :], 2)
+
+        @pl.when(c == 1)
+        def _():
+            sent(tower_all.at[pl.ds(0, 4 * depth), :], 2)
+
         sent(outbox.at[pl.ds(0, groups - 1)], 3)
         sent(pooled.at[pl.ds(0, 2)], 4)
 
@@ -460,12 +456,12 @@
     words = {
         "flip": flip,
         "widen": widen,
+        "WP": tower_pair,
         "WR": tower_relay,
         "WC": tower_corner,
-        "E": ready,
+        "E": ready_all,
         "Y": lift_first,
         "Z": lift_last,
-        "near": near_terms,
         "end": finish,
     }
     def follow(plan):
@@ -527,8 +523,8 @@
             pltpu.VMEM((rows, embed), jnp.float32),
             pltpu.VMEM((groups, rows, embed), jnp.bfloat16),
             pltpu.VMEM((members, groups, rows, embed), jnp.bfloat16),
-            pltpu.VMEM((members, rows * members, block), jnp.bfloat16),
-            pltpu.VMEM((members, rows * members, block), jnp.bfloat16),
+            pltpu.VMEM((rows * members, width), jnp.bfloat16),
+            pltpu.VMEM((rows * members, width), jnp.bfloat16),
             pltpu.VMEM((layers, width, rank), jnp.bfloat16),
             pltpu.VMEM((layers, block, rank), jnp.bfloat16),
             pltpu.VMEM((layers, members, rank, block), jnp.bfloat16),

time: 28.9 us -> 28.9 us (level)
  no operation moved by 1% of the time
where the time goes in v7:
time: 28.9 us; the launch traced here: 28.7 us
  Pallas kernels  28 us (97%)
  local copies, waits for them, and re-layouts  0.71 us (2%)
    pallas_call x1, Pallas kernels, fused_body(): pl.pallas_call(functools.partial(kernel, groups, members), out_shape=pltp...  28 us
    unnamed x1, local copies, waits for them, and re-layouts  0.71 us

profile of v7, /device:TPU:0, one launch (start us, length us, event | category | flops | bytes accessed | tf_op | source)
XLA Modules:
  0.0 28.7 jit_solution(12075436949804202166)
XLA Ops:
  0.0 28.0 %shard_map.82 = bf16[256,512]{1,0:T(8,128)(2,1)S(1)} custom-call(s32[16384]{0:T(1024)} %bitcast.6, s32[8]{0:T(128)} %order_hbm.1, bf16[1,4096,128]{2,1,0:T(8,128)(2,1)} %table.1, bf16[2,256,512]{2,1,0:T(8,128)(2,1)} %down.1, bf16[2,256,512]{2,1,0:T(8,128)(2,1)} %up.1, f32[2,256]{1,0:T(2,128)} %bias.1, bf16[128,512]{1,0:T(8,128)(2,1)} %tower.1, f32[1,512]{1,0:T(1,128)} %bitcast.7), custom_call_target="tpu_custom_call" | custom-call | tf_op jit(solution)/shard_map/pallas_call | solution.py:513
  28.0 0.7 %copy.10 = bf16[256,512]{1,0:T(8,128)(2,1)} copy(bf16[256,512]{1,0:T(8,128)(2,1)S(1)} %shard_map.82) | data formatting | bytes 524288

commit v8 on v6

--- a/solution.py
+++ b/solution.py
@@ -225,20 +225,21 @@
     def spread(p, k):
         mine = slot(p, came(k), d)
         arrived(mine, z_recv.at[p, k - 1])
-        send(mine, mine, p % 2, plane_recv.at[p, k - 1], chip_x * 2 + c, m)
-        send(mine, mine, p % 2, plane_recv.at[p, k - 1], chip_y * 2 + c, m)
+        send(mine, mine, p % 2, plane_recv.at[p, min(k, 2) - 1], chip_x * 2 + c, m)
+        send(mine, mine, p % 2, plane_recv.at[p, min(k, 2) - 1], chip_y * 2 + c, m)
         send(mine, mine, p % 2, pair_recv.at[p], partner, m)
 
     def pass_and_spread(p, k):
         mine = slot(p, came(k), d)
         arrived(mine, z_recv.at[p, k - 1])
         send(mine, mine, p % 2, z_recv.at[p, k - 1], d, beside)
-        send(mine, mine, p % 2, plane_recv.at[p, k - 1], chip_x * 2 + c, m)
-        send(mine, mine, p % 2, plane_recv.at[p, k - 1], chip_y * 2 + c, m)
+        send(mine, mine, p % 2, plane_recv.at[p, min(k, 2) - 1], chip_x * 2 + c, m)
+        send(mine, mine, p % 2, plane_recv.at[p, min(k, 2) - 1], chip_y * 2 + c, m)
         send(mine, mine, p % 2, pair_recv.at[p], partner, m)
 
     def relay(p, k):
-        arrived(amount(2), plane_recv.at[p, k - 1])
+        if k != 2:
+            arrived(amount(2 if k == 1 else 4), plane_recv.at[p, min(k, 2) - 1])
         for j in range(2):
             half = slot(p, came(k), chips[j] * 2 + c, j)
             send(half, half, p % 2, diag_recv.at[p], chips[1 - j] * 2 + c, m)
@@ -314,27 +315,26 @@
     def share_across(half):
         arrived(outbox.at[pl.ds(0, CHIPS - 1 + half)], pool_recv.at[half])
         mine = part(m, half)
-        send(mine, mine, 4, share_recv.at[m, half], d, across)
+        send(mine, mine, 4, share_recv.at[2 * place - 3 + half], d, across)
 
     def share_beside(half):
         mine = part(m, half)
-        send(mine, mine, 4, share_recv.at[m, half], d, beside)
+        send(mine, mine, 4, share_recv.at[0], d, beside)
 
     def pass_on(far, half):
         quarter = m + 2 - 4 * half_of if far else 3 - m
         theirs = part(quarter, half)
-        arrived(theirs, share_recv.at[quarter, half])
-        send(theirs, theirs, 4, share_recv.at[quarter, half], d, beside)
+        arrived(theirs, share_recv.at[(3 if far else 1) + half])
+        send(theirs, theirs, 4, share_recv.at[(3 if far else 1) + half], d, beside)
 
     def shared():
-        for half in range(2):
-            arrived(part(beside, half), share_recv.at[beside, half])
+        arrived(pooled.at[beside], share_recv.at[0])
 
         @pl.when(jnp.logical_not(inner))
         def _():
-            for j in range(2):
+            for quarter, first in ((across, 1), (outermost, 3)):
                 for half in range(2):
-                    arrived(part(far_first + j, half), share_recv.at[far_first + j, half])
+                    arrived(part(quarter, half), share_recv.at[first + half])
 
     def embed_all():
         per_block = block // embed
@@ -538,12 +538,12 @@
             dma((8,)),
             dma((6,)),
             dma((pieces, members - 1)),
-            dma((pieces, members - 1)),
+            dma((pieces, 2)),
             dma((pieces,)),
             dma((pieces,)),
             dma((4,)),
             dma((2,)),
-            dma((members, 2)),
+            dma((5,)),
             dma((1,)),
         ],
         compiler_params=pltpu.CompilerParams(

time: 28.9 us -> 28.8 us (level)
  no operation moved by 1% of the time
where the time goes in v8:
time: 28.8 us; the launch traced here: 28.7 us
  Pallas kernels  28 us (97%)
  local copies, waits for them, and re-layouts  0.71 us (2%)
    pallas_call x1, Pallas kernels, fused_body(): pl.pallas_call(functools.partial(kernel, groups, members), out_shape=pltp...  28 us
    unnamed x1, local copies, waits for them, and re-layouts  0.71 us

profile of v8, /device:TPU:0, one launch (start us, length us, event | category | flops | bytes accessed | tf_op | source)
XLA Modules:
  0.0 28.7 jit_solution(10422759112740128225)
XLA Ops:
  0.0 28.0 %shard_map.82 = bf16[256,512]{1,0:T(8,128)(2,1)S(1)} custom-call(s32[16384]{0:T(1024)} %bitcast.6, s32[8]{0:T(128)} %order_hbm.1, bf16[1,4096,128]{2,1,0:T(8,128)(2,1)} %table.1, bf16[2,256,512]{2,1,0:T(8,128)(2,1)} %down.1, bf16[2,256,512]{2,1,0:T(8,128)(2,1)} %up.1, f32[2,256]{1,0:T(2,128)} %bias.1, bf16[128,512]{1,0:T(8,128)(2,1)} %tower.1, f32[1,512]{1,0:T(1,128)} %bitcast.7), custom_call_target="tpu_custom_call" | custom-call | tf_op jit(solution)/shard_map/pallas_call | solution.py:517
  28.0 0.7 %copy.10 = bf16[256,512]{1,0:T(8,128)(2,1)} copy(bf16[256,512]{1,0:T(8,128)(2,1)S(1)} %shard_map.82) | data formatting | bytes 524288
